TPU v7x, 32 devices: a whole 2x2x4 slice. The times are simulated.
32 devices in a mesh: pop: 2 (over x), snp: 16 (over z, y, core).
Axes of the slice: x: 2, y: 2, z: 4, core: 2. Of those that a mesh axis runs over, the one named last changes fastest.
Arguments:
- genotypes: float32 [4, 1024, 16384], P('pop', None, 'snp'), may hold values from -6 to 6
- pop_id: int32 [4], replicated, may hold values from 0 to 4
- window: int32 [1], replicated, may hold values from 512 to 1024
- tile_counts: int32 [128], P('snp'), may hold values from 64 to 128
- weights: float32 [5, 128], replicated, may hold values from 0.1 to 1
Outputs:
- combined: float32 [16384, 1024], P(('snp', 'pop'))
All inputs are finite; a program needn't handle non-finite values.
Results may differ from a plain program's by a relative error of at most 0.000067.
Values sent between devices are 32-bit elements; how exact they have to be, the bound alone decides.
No kernel may reach another device: no remote copies, remote signals or barrier semaphores. Data moves between devices by JAX's collectives and lax.ppermute only.
A program may use at most 128 MiB of HBM per device.

v0:
```python
import jax
import jax.numpy as jnp
from jax import lax
from jax.sharding import PartitionSpec as P

WIN = 1024
NPOPS = 5


def from_behind(block, axis, distance):
    devices = range(lax.axis_size(axis))
    route = [(i - distance, i) for i in devices if i - distance in devices]
    return lax.ppermute(block, axis, route)


def skewed(panel):
    lead = panel.shape[:-2]
    height = panel.shape[-2]
    span = panel.shape[-1] - height
    flat = panel.reshape(lead + (height * (height + span),))
    flat = jnp.concatenate([flat, jnp.zeros(lead + (height,), panel.dtype)], axis=-1)
    return flat.reshape(lead + (height, height + span + 1))[..., :span]


def shards(genotypes, pop_id, window, tile_counts, weights):
    cohorts_dev, people, snp_dev = genotypes.shape
    tiles_dev = snp_dev // 128
    groups = lax.axis_size("pop")
    group = lax.axis_index("pop")
    valid = (tile_counts[:, None] > jnp.arange(128, dtype=jnp.int32)[None, :]).astype(jnp.float32)
    masked = genotypes * valid.reshape(snp_dev)
    ahead = from_behind(masked, "snp", -1)
    extended = jnp.concatenate([masked, ahead], axis=2)
    onehot = (pop_id[:, None] == jnp.arange(NPOPS, dtype=jnp.int32)[None, :]).astype(jnp.float32)
    per_cohort = jnp.dot(
        onehot, weights, precision=lax.Precision.HIGHEST, preferred_element_type=jnp.float32
    )
    coef_all = per_cohort / jnp.sum(per_cohort, axis=0, keepdims=True)
    coef_local = lax.dynamic_slice_in_dim(coef_all, lax.axis_index("snp") * tiles_dev, tiles_dev, 1)
    keep = (jnp.arange(WIN, dtype=jnp.int32) < window[0]).astype(jnp.float32)
    own_coef = lax.dynamic_slice_in_dim(coef_local, group * cohorts_dev, cohorts_dev, 0)
    count = lax.axis_size("pop") * (snp_dev // groups)

    def one_tile(tile_index):
        panel = lax.dynamic_slice_in_dim(extended, tile_index * 128, 128 + WIN, 2)
        products = (
            jnp.einsum("cki,ckj->cij", panel[:, :, :128], panel, precision=lax.Precision.HIGHEST)
            / people
        )
        return skewed(products) * keep

    band_part = lax.map(one_tile, jnp.arange(count // 128, dtype=jnp.int32))
    return lax.psum_scatter(
        jnp.sum(own_coef.T[:, :, None, None] * band_part, axis=1).reshape(count, WIN),
        "pop",
        scatter_dimension=0,
        tiled=True,
    )


def solution(mesh):
    return jax.shard_map(
        shards,
        mesh=mesh,
        in_specs=(P("pop", None, "snp"), P(), P(), P("snp"), P()),
        out_specs=P(("snp", "pop"), None),
        check_vma=False,
    )
```

profile of v0, /device:TPU:0, one launch (start us, length us, event | category | flops | bytes accessed | tf_op | source)
XLA Modules:
  0.0 317.2 jit_solution(12906286109319728504)
XLA Ops:
  6.5 0.7 convert_bitcast_fusion
  7.3 8.5 %broadcast_multiply_fusion = f32[2,1024,1024]{2,1,0:T(8,128)} fusion(f32[2,1024,1024]{2,1,0:T(8,128)} %param.7, f32[1024]{0:T(1024)S(1)} %convert_bitcast_fusion), kind=kLoop, calls=%fused_computation.14 | loop fusion | flops 2097152 | bytes 16781312 | tf_op jit(solution)/shard_map/mul | solution.py:31
  15.8 1.3 collective-permute-start
  17.5 13.7 %collective-permute-done = f32[2,1024,1024]{2,1,0:T(8,128)} collective-permute-done((f32[2,1024,1024]{2,1,0:T(8,128)}, f32[2,1024,1024]{2,1,0:T(8,128)}, u32[]{:S(2)}, u32[]{:S(2)}) %collective-permute-start) | collective-permute-done | bytes 8388640 | tf_op jit(solution)/shard_map/ppermute | solution.py:13
  31.2 11.7 %pad_maximum_fusion = f32[2,1024,2048]{2,1,0:T(8,128)} fusion(f32[2,1024,1024]{2,1,0:T(8,128)} %collective-permute-done, f32[2,1024,1024]{2,1,0:T(8,128)} %broadcast_multiply_fusion), kind=kLoop, calls=%fused_computation.12 | loop fusion | flops 4194304 | bytes 33554432 | tf_op jit(solution)/shard_map/concatenate | solution.py:33
  42.9 124.0 %while.11 = (s32[]{:T(128)}, f32[8,2,128,1024]{3,2,1,0:T(8,128)}, s32[8]{0:T(128)S(1)}, f32[2,1024,2048]{2,1,0:T(8,128)}, s32[]{:T(128)}, /*index=5*/s32[]{:T(128)}, s32[1]{0:T(128)}, s32[]{:T(128)}, s32[]{:T(128)}, f32[]{:T(128)}) while((s32[]{:T(128)}, f32[8,2,128,1024]{3,2,1,0:T(8,128)}, s32[8]{0:T(128)S(1)}, ...), condition=%wide.region_2.3_spmd.clone, body=%wide.region_1.2_spmd.clone.sunk | while | flops 3624437760 | bytes 20853416 | solution.py:52
  44.1 9.6 %fusion.26 = f32[1,2,128,1152]{3,2,1,0:T(8,128)S(1)} fusion(f32[2,1024,2048]{2,1,0:T(8,128)} %get-tuple-element.112, s32[]{:T(128)S(6)} %select_n.19), kind=kOutput, calls=%fused_computation.4.clone.1 | convolution fusion | flops 3624173568 | bytes 11666432 | tf_op jit(solution)/shard_map/while/body/eval_jaxpr/cki,ckj->cij/dot_general | solution.py:47
  53.7 0.9 copy.13
  55.1 1.5 reshape.38
  56.6 0.7 fusion.27
  57.2 1.1 fusion.28
  59.6 9.6 %fusion.26 = f32[1,2,128,1152]{3,2,1,0:T(8,128)S(1)} fusion(f32[2,1024,2048]{2,1,0:T(8,128)} %get-tuple-element.112, s32[]{:T(128)S(6)} %select_n.19), kind=kOutput, calls=%fused_computation.4.clone.1 | convolution fusion | flops 3624173568 | bytes 11666432 | tf_op jit(solution)/shard_map/while/body/eval_jaxpr/cki,ckj->cij/dot_general | solution.py:47
  69.2 0.9 copy.13
  70.6 1.5 reshape.38
  72.1 0.7 fusion.27
  72.7 1.2 fusion.28
  75.1 9.6 %fusion.26 = f32[1,2,128,1152]{3,2,1,0:T(8,128)S(1)} fusion(f32[2,1024,2048]{2,1,0:T(8,128)} %get-tuple-element.112, s32[]{:T(128)S(6)} %select_n.19), kind=kOutput, calls=%fused_computation.4.clone.1 | convolution fusion | flops 3624173568 | bytes 11666432 | tf_op jit(solution)/shard_map/while/body/eval_jaxpr/cki,ckj->cij/dot_general | solution.py:47
  84.7 0.9 copy.13
  86.1 1.5 reshape.38
  87.6 0.7 fusion.27
  88.3 1.1 fusion.28
  90.6 9.6 %fusion.26 = f32[1,2,128,1152]{3,2,1,0:T(8,128)S(1)} fusion(f32[2,1024,2048]{2,1,0:T(8,128)} %get-tuple-element.112, s32[]{:T(128)S(6)} %select_n.19), kind=kOutput, calls=%fused_computation.4.clone.1 | convolution fusion | flops 3624173568 | bytes 11666432 | tf_op jit(solution)/shard_map/while/body/eval_jaxpr/cki,ckj->cij/dot_general | solution.py:47
  100.2 0.9 copy.13
  101.6 1.5 reshape.38
  103.1 0.7 fusion.27
  103.8 1.1 fusion.28
  106.1 9.6 %fusion.26 = f32[1,2,128,1152]{3,2,1,0:T(8,128)S(1)} fusion(f32[2,1024,2048]{2,1,0:T(8,128)} %get-tuple-element.112, s32[]{:T(128)S(6)} %select_n.19), kind=kOutput, calls=%fused_computation.4.clone.1 | convolution fusion | flops 3624173568 | bytes 11666432 | tf_op jit(solution)/shard_map/while/body/eval_jaxpr/cki,ckj->cij/dot_general | solution.py:47
  115.7 0.9 copy.13
  117.1 1.5 reshape.38
  118.6 0.7 fusion.27
  119.3 1.1 fusion.28
  121.6 9.6 %fusion.26 = f32[1,2,128,1152]{3,2,1,0:T(8,128)S(1)} fusion(f32[2,1024,2048]{2,1,0:T(8,128)} %get-tuple-element.112, s32[]{:T(128)S(6)} %select_n.19), kind=kOutput, calls=%fused_computation.4.clone.1 | convolution fusion | flops 3624173568 | bytes 11666432 | tf_op jit(solution)/shard_map/while/body/eval_jaxpr/cki,ckj->cij/dot_general | solution.py:47
  131.2 0.9 copy.13
  132.6 1.5 reshape.38
  134.1 0.7 fusion.27
  134.7 1.2 fusion.28
  137.1 9.6 %fusion.26 = f32[1,2,128,1152]{3,2,1,0:T(8,128)S(1)} fusion(f32[2,1024,2048]{2,1,0:T(8,128)} %get-tuple-element.112, s32[]{:T(128)S(6)} %select_n.19), kind=kOutput, calls=%fused_computation.4.clone.1 | convolution fusion | flops 3624173568 | bytes 11666432 | tf_op jit(solution)/shard_map/while/body/eval_jaxpr/cki,ckj->cij/dot_general | solution.py:47
  146.7 0.9 copy.13
  148.1 1.5 reshape.38
  149.6 0.7 fusion.27
  150.3 1.1 fusion.28
  152.6 9.6 %fusion.26 = f32[1,2,128,1152]{3,2,1,0:T(8,128)S(1)} fusion(f32[2,1024,2048]{2,1,0:T(8,128)} %get-tuple-element.112, s32[]{:T(128)S(6)} %select_n.19), kind=kOutput, calls=%fused_computation.4.clone.1 | convolution fusion | flops 3624173568 | bytes 11666432 | tf_op jit(solution)/shard_map/while/body/eval_jaxpr/cki,ckj->cij/dot_general | solution.py:47
  162.2 0.9 copy.13
  163.6 1.5 reshape.38
  165.1 0.7 fusion.27
  165.8 1.1 fusion.28
  166.9 7.1 %multiply_reduce_fusion = f32[8,128,1024]{2,1,0:T(8,128)} fusion(f32[8,2,128,1024]{3,2,1,0:T(8,128)} %get-tuple-element.32, f32[8,2]{1,0:T(8,128)S(1)} %copy.9), kind=kLoop, calls=%fused_computation.13 | loop fusion | flops 3145728 | bytes 12582976 | tf_op jit(solution)/shard_map/reduce_sum | solution.py:54
  174.0 136.3 %reduce-scatter.2.cloned.1.call-done = f32[512,1024]{1,0:T(8,128)} async-done(((f32[1024,1024]{1,0:T(8,128)}), f32[512,1024]{1,0:T(8,128)}) %reduce-scatter.2.cloned.1.call-update) | async-done | bytes 2097168 | tf_op jit(solution)/shard_map/reduce_scatter | solution.py:53
  (28 shorter events, 8.9 us)
Async XLA Ops:
  6.5 10.6 %copy-start = (f32[5,128]{1,0:T(8,128)S(1)}, f32[5,128]{1,0:T(8,128)}, u32[]{:S(2)}) copy-start(f32[5,128]{1,0:T(8,128)} %param.11) | copy-start | bytes 7684
  6.5 303.8 %reduce-scatter.2.cloned.1.call-start = ((), (), s32[]{:S(2)}) async-start(), calls=%async_computation.1 | async-start | bytes 6291456 | tf_op jit(solution)/shard_map/reduce_scatter | solution.py:53
  7.3 9.9 %copy-start.1 = (s32[4]{0:T(128)S(1)}, s32[4]{0:T(128)}, u32[]{:S(2)}) copy-start(s32[4]{0:T(128)} %param.8) | copy-start | bytes 52
  15.8 15.4 %collective-permute-start = (f32[2,1024,1024]{2,1,0:T(8,128)}, f32[2,1024,1024]{2,1,0:T(8,128)}, u32[]{:S(2)}, u32[]{:S(2)}) collective-permute-start(f32[2,1024,1024]{2,1,0:T(8,128)} %broadcast_multiply_fusion), channel_id=1, source_target_pairs={{1,0},{2,1},{3,2},{4,3},{5,4},{6,5},{7,6},{8,7},{9,8},{10,9},{11,1... | collective-permute-start | bytes 25165832 | tf_op jit(solution)/shard_map/ppermute | solution.py:13
Sparse Core Ops, SparseCore 0:
  174.1 136.1 reduce-scatter.1
where the time goes:
time: 318 us; the launch traced here: 317 us
  waiting for transfers between devices  150 us (47%)
  matrix products  76.6 us (24%)
  other arithmetic  42.3 us (13%)
  local copies, waits for them, and re-layouts  28.1 us (9%)
  between operations  13.4 us (4%)
  loops' own time  5.39 us (2%)
    reduce_scatter x1, waiting for transfers between devices, shards(): lax.psum_scatter(jnp.sum(own_coef.T[:, :, None, None] * band_part, axis=1...  136 us
    dot_general x8, matrix products, one_tile(): jnp.einsum('cki,ckj->cij', panel[:, :, :128], panel, precision=lax.Precis...  76.4 us
    ppermute x1, waiting for transfers between devices, from_behind(): return lax.ppermute(block, axis, route)  13.7 us
    reshape x8, local copies, waits for them, and re-layouts, skewed(): return flat.reshape(lead + (height, height + span + 1))[..., :span]  12.1 us
    concatenate x1, other arithmetic, shards(): extended = jnp.concatenate([masked, ahead], axis=2)  11.7 us
    dynamic_update_slice x8, other arithmetic, shards(): band_part = lax.map(one_tile, jnp.arange(count // 128, dtype=jnp.int32))  9.12 us
    mul x1, other arithmetic, shards(): masked = genotypes * valid.reshape(snp_dev)  8.53 us
    while x8, local copies, waits for them, and re-layouts  7.3 us
  transfers between devices with their start and end apart: 2, of which 2 were waited for; matrix products, arithmetic and copies ran while one was open for 0% of the time, Pallas kernels for 0%

commit v1 on v0

v1 whole, which is shorter than its diff:
```python
import functools

import jax
import jax.numpy as jnp
from jax import lax
from jax.experimental import pallas as pl
from jax.experimental.pallas import tpu as pltpu
from jax.sharding import PartitionSpec as P


WIN = 1024
TILE = 128
STRIP = 256
F32 = jnp.float32
BF16 = jnp.bfloat16
SMEM = pl.BlockSpec(memory_space=pltpu.SMEM)
VMEM = pl.BlockSpec(memory_space=pltpu.VMEM)
PARAMS = pltpu.CompilerParams(vmem_limit_bytes=20 * 2**20)
HOPS = {8: (2, 2, 2, 1, 1), 7: (2, 2, 2, 1), 6: (2, 2, 1, 1), 5: (2, 2, 1)}


class Hop:
    def __init__(self, tile, wide, steps, tiles):
        self.tile, self.wide = tile, wide
        self.first = tile + tiles - steps
        self.base = max(self.first, tiles // 2)
        self.top = max(0, tiles // 2 - self.first) * wide
        self.bottom = (tiles - self.base) * wide
        self.rest = (0, 0)


class Plan:
    def __init__(self, steps, tiles):
        self.steps, self.tiles, self.half = steps, tiles, tiles // 2
        self.counts = [min(steps + 1, tiles - r) for r in range(tiles)]
        starts = [sum(self.counts[:r]) for r in range(tiles + 1)]
        self.n0 = starts[self.half]
        self.n1 = starts[tiles] - self.n0
        self.starts = [s if r < self.half else s - self.n0 for r, s in enumerate(starts[:tiles])]
        self.hops, tile = [], 0
        for wide in HOPS[steps]:
            self.hops.append(Hop(tile, wide, steps, tiles))
            tile += wide
        spare = sum(max(0, hop.bottom - hop.top) for hop in self.hops[:-1])
        self.first_swap = max(self.n1, self.n0 - spare)
        left = self.first_swap
        for hop in self.hops[:-1]:
            take = max(0, min(self.n0 - left, hop.bottom - hop.top))
            hop.rest = (left, take)
            hop.swap = max(hop.bottom, hop.top + take)
            left += take


def split(x):
    high = x.astype(BF16)
    return high, (x - high.astype(F32)).astype(BF16)


def pick(row, values):
    result = values[0]
    for r, value in enumerate(values[1:], 1):
        result = jnp.where(row == r, value, result)
    return result


def own_kernel(plan, counts, pops, table, g_ref, ah, al, own0, own1, send, high, low):
    cohorts, people, span = g_ref.shape
    wide = span // TILE
    step = pl.program_id(0)
    group = lax.axis_index("pop")
    lane = lax.broadcasted_iota(jnp.int32, (1, TILE), 1)
    for w in range(wide):
        t = step * wide + w
        place = lax.axis_index("snp") * plan.tiles + t
        mask = (lane < counts[t]).astype(F32)
        total = table[pops[0], place]
        for e in range(1, pops.shape[0]):
            total = total + table[pops[e], place]
        rows = pl.ds(pl.multiple_of(t * TILE, TILE), TILE)
        columns = slice(w * TILE, (w + 1) * TILE)

        def prepare(i, carry):
            c, k = i // (people // STRIP), i % (people // STRIP)
            deep = pl.ds(pl.multiple_of(i * STRIP, STRIP), STRIP)
            x = g_ref[c, pl.ds(pl.multiple_of(k * STRIP, STRIP), STRIP), columns] * mask
            high[deep, columns], low[deep, columns] = split(x)
            share = table[pops[group * cohorts + c], place]
            coef = jnp.full((1, TILE), share, F32) / jnp.full((1, TILE), total, F32) * (1.0 / people)
            ah[rows, deep], al[rows, deep] = split((x * coef).T)
            return carry

        lax.fori_loop(0, cohorts * people // STRIP, prepare, 0)

    def block(q, carry):
        rows = pl.ds(pl.multiple_of(q * span, span), span)
        prod = jnp.dot(ah[rows, :], high[...], preferred_element_type=F32)
        prod = prod + jnp.dot(ah[rows, :], low[...], preferred_element_type=F32)
        prod = prod + jnp.dot(al[rows, :], high[...], preferred_element_type=F32)
        for k in range(wide):
            row = q * wide + k
            start = pick(row, plan.starts)
            for w in range(wide):
                m = step * wide + w - row
                spot = start + m
                inside = (m >= 0) & (m <= plan.steps)
                tile = prod[k * TILE : (k + 1) * TILE, w * TILE : (w + 1) * TILE]

                @pl.when(inside & (row < plan.half))
                def _():
                    own0[spot] = tile

                @pl.when(inside & (row >= plan.half))
                def _():
                    own1[spot] = tile

                @pl.when(inside & ((row < plan.half) == (group == 1)) & (spot < plan.first_swap))
                def _():
                    send[spot] = tile

        return carry

    lax.fori_loop(jnp.maximum(step * wide - plan.steps, 0) // wide, step + 1, block, 0)


def own_part(plan, genotypes, tile_counts, pop_id, weights):
    cohorts, people, snps = genotypes.shape
    deep = cohorts * people
    span = 2 * TILE
    tall = jax.ShapeDtypeStruct((snps, deep), BF16)
    sizes = (plan.n0, plan.n1, plan.first_swap)
    return pl.pallas_call(
        functools.partial(own_kernel, plan),
        grid=(snps // span,),
        in_specs=[SMEM, SMEM, SMEM, pl.BlockSpec((cohorts, people, span), lambda t: (0, 0, t))],
        out_specs=[VMEM] * 5,
        out_shape=[tall, tall] + [jax.ShapeDtypeStruct((n, TILE, TILE), F32) for n in sizes],
        scratch_shapes=[pltpu.VMEM((deep, span), BF16), pltpu.VMEM((deep, span), BF16)],
        cost_estimate=pl.CostEstimate(
            flops=6 * deep * snps * snps * 5 // 8, bytes_accessed=4 * deep * snps, transcendentals=0
        ),
        compiler_params=PARAMS,
    )(tile_counts, pop_id, weights, genotypes)


def hop_kernel(plan, hop, got, ah, al, *refs):
    refs = list(refs)
    own0 = refs.pop(0) if hop.rest[1] else None
    top = refs.pop(0) if hop.top else None
    bottom = refs.pop(0)
    low, high = refs.pop(), refs.pop()
    send = refs.pop() if refs else None
    group = lax.axis_index("pop")
    wide = hop.wide
    people = got.shape[1]

    def prepare(i, carry):
        c, k = i // (people // STRIP), i % (people // STRIP)
        deep = pl.ds(pl.multiple_of(i * STRIP, STRIP), STRIP)
        high[deep, :], low[deep, :] = split(got[c, pl.ds(pl.multiple_of(k * STRIP, STRIP), STRIP), :])
        return carry

    lax.fori_loop(0, got.shape[0] * people // STRIP, prepare, 0)

    def block(row, tall):
        rows = pl.ds(pl.multiple_of(row * TILE, TILE), tall * TILE)
        if wide == 1:
            both = jnp.concatenate([high[...], low[...]], axis=1)
            prod = jnp.dot(ah[rows, :], both, preferred_element_type=F32)
            prod = prod[:, :TILE] + prod[:, TILE:]
        else:
            prod = jnp.dot(ah[rows, :], high[...], preferred_element_type=F32)
            prod = prod + jnp.dot(ah[rows, :], low[...], preferred_element_type=F32)
        prod = prod + jnp.dot(al[rows, :], high[...], preferred_element_type=F32)
        for k in range(tall):

            def put(out, base, owner):
                for w in range(wide):
                    tile = prod[k * TILE : (k + 1) * TILE, w * TILE : (w + 1) * TILE]
                    spot = (row + k - base) * wide + w
                    out[spot] = tile
                    if send is not None:

                        @pl.when(group == owner)
                        def _():
                            send[spot] = tile

            if top is not None:
                upper = (row + k >= hop.first) & (row + k < plan.half)
                pl.when(upper)(functools.partial(put, top, hop.first, 1))
            pl.when(row + k >= hop.base)(functools.partial(put, bottom, hop.base, 0))

    even = hop.first // 2

    def pair(q, carry):
        block(2 * q, 2)
        return carry

    if plan.tiles - hop.first > 1:
        lax.fori_loop(even, plan.tiles // 2, pair, 0)
    else:
        block(hop.first, 1)
    if hop.rest[1]:

        @pl.when(group == 1)
        def _():
            send[hop.top : hop.top + hop.rest[1]] = own0[hop.rest[0] : hop.rest[0] + hop.rest[1]]


def hop_part(plan, hop, got, ah, al, own0, tag):
    deep = ah.shape[1]
    span = hop.wide * TILE
    args = [got, ah, al] + ([own0] if hop.rest[1] else [])
    sizes = ([hop.top] if hop.top else []) + [hop.bottom] + ([hop.swap] if tag + 1 < len(plan.hops) else [])
    outs = pl.pallas_call(
        functools.partial(hop_kernel, plan, hop),
        in_specs=[VMEM] * len(args),
        out_specs=[VMEM] * len(sizes),
        out_shape=[jax.ShapeDtypeStruct((n, TILE, TILE), F32) for n in sizes],
        scratch_shapes=[pltpu.VMEM((deep, span), BF16), pltpu.VMEM((deep, span), BF16)],
        cost_estimate=pl.CostEstimate(
            flops=6 * deep * span * (plan.tiles - hop.first) * TILE,
            bytes_accessed=4 * deep * span,
            transcendentals=0,
        ),
        compiler_params=PARAMS,
    )(*args)
    outs = list(outs)
    top = outs.pop(0) if hop.top else None
    return top, outs[0], outs[-1]


def skew(tile):
    groups = [tile[g : g + 8] for g in range(0, TILE, 8)]
    tile = jnp.concatenate([pltpu.roll(x, (TILE - 8 * g) % TILE, 1) if g else x for g, x in enumerate(groups)], axis=0)
    row = lax.broadcasted_iota(jnp.int32, (TILE, TILE), 0)
    for bit in (1, 2, 4):
        tile = jnp.where((row & bit) != 0, pltpu.roll(tile, TILE - bit, 1), tile)
    return tile


def band_tile(this, after, step, window):
    lane = lax.broadcasted_iota(jnp.int32, (TILE, TILE), 1)
    row = lax.broadcasted_iota(jnp.int32, (TILE, TILE), 0)
    mixed = jnp.where(lane + row < TILE, this, after)
    return jnp.where(step * TILE + lane < window, mixed, 0.0)


def runs(plan, h, r, own, swapped, parts):
    row = h * plan.half + r
    start, count = plan.starts[row], plan.counts[row]
    result = []
    edges = [(swapped, 0, plan.first_swap, 0)]
    if h == 0:
        edges += [(part[2], hop.rest[0], hop.rest[1], hop.top) for hop, part in zip(plan.hops, parts)]
    for came, begin, length, base in edges:
        lo, hi = max(start, begin), min(start + count, begin + length)
        if lo < hi:
            result.append((own[h], lo, came, base + lo - begin, lo - start, hi - lo))
    for hop, (top, bottom, came) in zip(plan.hops, parts):
        if row < hop.first:
            continue
        step = plan.tiles + hop.tile - row
        spot = (row - (hop.base if h else hop.first)) * hop.wide
        result.append((bottom if h else top, spot, came, spot, step, min(hop.wide, plan.steps + 1 - step)))
    return result


def finish_kernel(plan, window, own0, own1, swapped, *refs):
    refs = list(refs)
    band = refs.pop()
    out = refs.pop()
    parts = []
    for hop in plan.hops[:-1]:
        top = refs.pop(0) if hop.top else None
        parts.append((top, refs.pop(0), refs.pop(0)))
    group = lax.axis_index("pop")
    for h in range(2):

        @pl.when(group == h)
        def _():
            for r in range(plan.half):
                for kept, a, came, b, step, count in runs(plan, h, r, (own0, own1), swapped, parts):

                    def add(i, carry, r=r, kept=kept, a=a, came=came, b=b, step=step):
                        band[r, step + i] = kept[a + i] + came[b + i]
                        return carry

                    lax.fori_loop(0, count, add, 0)

    def line(r, carry):
        rows = pl.ds(pl.multiple_of(r * TILE, TILE), TILE)
        this = skew(band[r, 0])
        for m in range(plan.steps):
            after = skew(band[r, m + 1])
            out[rows, m * TILE : (m + 1) * TILE] = band_tile(this, after, m, window[0])
            this = after
        if plan.steps * TILE < out.shape[1]:
            out[rows, plan.steps * TILE :] = jnp.zeros((TILE, out.shape[1] - plan.steps * TILE), F32)
        return carry

    lax.fori_loop(0, plan.half, line, 0)


def last_kernel(plan, window, old, k0, k1, c0, c1, out):
    this = skew(k0[k0.shape[0] - 1] + c0[plan.hops[-2].bottom - 1])
    after = skew(k1[0] + c1[0])
    fresh = band_tile(this, after, plan.steps - 1, window[0])
    out[...] = jnp.where(lax.axis_index("pop") == 1, fresh, old[...])


def band(steps, genotypes, pop_id, window, tile_counts, weights):
    snps = genotypes.shape[2]
    tiles = snps // TILE
    half = tiles // 2
    assert snps == WIN and tiles % 2 == 0 and lax.axis_size("pop") == 2
    plan = Plan(steps, tiles)
    valid = (tile_counts[:, None] > jnp.arange(TILE, dtype=jnp.int32)[None, :]).astype(F32).reshape(snps)
    behind = [(i + 1, i) for i in range(lax.axis_size("snp") - 1)]

    def swap(block, route):
        return lax.ppermute(block, "pop", route)

    arrivals = []
    for j, hop in enumerate(plan.hops):
        if j == 2:
            ah, al, own0, own1, send = own_part(plan, genotypes, tile_counts, pop_id, weights)
            valid, send, piece = lax.optimization_barrier((valid, send, piece))
        elif j:
            valid, piece = lax.optimization_barrier((valid, piece))
        span = slice(hop.tile * TILE, (hop.tile + hop.wide) * TILE)
        piece = genotypes[:, :, span] * valid[span]
        arrivals.append(lax.ppermute(piece, "snp", behind))
    both = [(0, 1), (1, 0)]
    swapped = swap(send, both)
    parts = []
    for j, (hop, got) in enumerate(zip(plan.hops, arrivals)):
        top, bottom, send = hop_part(plan, hop, got, ah, al, own0, j)
        route = both if hop.top or hop.rest[1] else both[:1]
        parts.append((top, bottom, swap(send, route)))
    lists = [own0, own1, swapped]
    for part in parts[:-1]:
        lists += [x for x in part if x is not None]
    shape = jax.ShapeDtypeStruct((half * TILE, WIN), F32)
    finish = pl.pallas_call(
        functools.partial(finish_kernel, plan),
        in_specs=[SMEM] + [VMEM] * len(lists),
        out_specs=VMEM,
        out_shape=shape,
        scratch_shapes=[pltpu.VMEM((half, steps + 1, TILE, TILE), F32)],
        cost_estimate=pl.CostEstimate(flops=10**9, bytes_accessed=6 * half * TILE * WIN * 4, transcendentals=0),
        compiler_params=PARAMS,
    )
    out = finish(window, *lists)
    corner = pl.BlockSpec((TILE, TILE), lambda i: (half - 1, steps - 1))
    return pl.pallas_call(
        functools.partial(last_kernel, plan),
        grid=(1,),
        in_specs=[SMEM, corner, VMEM, VMEM, VMEM, VMEM],
        out_specs=corner,
        out_shape=shape,
        input_output_aliases={1: 0},
        cost_estimate=pl.CostEstimate(flops=10**7, bytes_accessed=6 * TILE * TILE * 4, transcendentals=0),
        compiler_params=PARAMS,
    )(window, out, parts[-2][1], parts[-1][1], parts[-2][2], parts[-1][2])


def solution(mesh):
    sizes = sorted(HOPS)

    def branch(steps):
        def body(*args):
            return band(steps, *args)

        return body

    def body(genotypes, pop_id, window, tile_counts, weights):
        steps = (window[0] + TILE - 1) // TILE
        return lax.switch(
            jnp.clip(steps - sizes[0], 0, len(sizes) - 1),
            [branch(n) for n in sizes],
            genotypes,
            pop_id,
            window,
            tile_counts,
            weights,
        )

    return jax.shard_map(
        body,
        mesh=mesh,
        in_specs=(P("pop", None, "snp"), P(), P(), P("snp"), P()),
        out_specs=P(("snp", "pop"), None),
        check_vma=False,
    )
```

time: 318 us -> 79.4 us (0.25)
  the two profiles are of different devices: /device:TPU:0 before, /device:TPU:18 now
where the time goes in v1:
time: 79.4 us; the launch traced here: 79.1 us
  Pallas kernels  33.9 us (43%)
  waiting for transfers between devices  28.2 us (36%)
  starting transfers between devices  11.5 us (14%)
  other arithmetic  4.51 us (6%)
    ppermute x3, waiting for transfers between devices, band(): arrivals.append(lax.ppermute(piece, 'snp', behind))  22.4 us
    pallas_call x1, Pallas kernels, own_part(): pl.pallas_call(functools.partial(own_kernel, plan), grid=(snps // span,),...  19.7 us
    ppermute x3, starting transfers between devices, band(): arrivals.append(lax.ppermute(piece, 'snp', behind))  7.52 us
    pallas_call x3, Pallas kernels, hop_part(): pl.pallas_call(functools.partial(hop_kernel, plan, hop), in_specs=[VMEM]...  6.46 us
    ppermute x4, waiting for transfers between devices, swap(): return lax.ppermute(block, 'pop', route)  5.85 us
    pallas_call x1, Pallas kernels, band(): out = finish(window, *lists)  5.32 us
    ppermute x4, starting transfers between devices, swap(): return lax.ppermute(block, 'pop', route)  4.03 us
    mul x4, other arithmetic, band(): piece = genotypes[:, :, span] * valid[span]  3.78 us
  transfers between devices with their start and end apart: 7, of which 3 were waited for; matrix products, arithmetic and copies ran while one was open for 2% of the time, Pallas kernels for 40%

profile of v1, /device:TPU:18, one launch (start us, length us, event | category | flops | bytes accessed | tf_op | source)
XLA Modules:
  0.0 79.1 jit_solution(12543939565769987942)
XLA Ops:
  0.7 78.4 %conditional.1 = (f32[512,1024]{1,0:T(8,128)}) conditional(s32[]{:T(128)} %clamp.3, (s32[8]{0:T(128)}, s32[4]{0:T(128)}, f32[5,128]{1,0:T(8,128)}, f32[2,1024,1024]{2,1,0:T(8,128)}, s32[1]{0:T(128)}) %tuple.29, (s32[8]{0:T(128)}, s32[4]{0:T(128)}, f32[5,128]{1,0:T(8,128)}, f32[2,1024,1024]{2,1,0:T(8,128)}, ...), branch_computations={%region_0.1_spmd, %region_1.2_spmd, %region_2.3_spmd, %region_3.4_... | conditional | flops 16916899840 | bytes 123890704 | solution.py:378
  0.7 0.7 iota_compare_fusion
  1.4 0.0 copy-start
  1.4 1.9 %slice_multiply_fusion.1 = f32[2,1024,256]{2,1,0:T(8,128)S(1)} fusion(f32[2,1024,1024]{2,1,0:T(8,128)} %get-tuple-element.165.g_ref, f32[256]{0:T(256)S(1)} %fusion), kind=kLoop, calls=%fused_computation.1 | loop fusion | flops 524288 | bytes 4195328 | tf_op jit(solution)/shard_map/cond/branch_0_fun/mul | solution.py:331
  3.3 3.0 %collective-permute-start.1 = (f32[2,1024,256]{2,1,0:T(8,128)S(1)}, f32[2,1024,256]{2,1,0:T(8,128)S(1)}, u32[]{:S(2)}, u32[]{:S(2)}) collective-permute-start(f32[2,1024,256]{2,1,0:T(8,128)S(1)} %slice_multiply_fusion.1), channel_id=1, source_target_pairs={{1,0},{2,1},{3,2},{4,3},{5,4},{6,5},{7,6},{8,7},{9,8},{10,9},{11,1... | collective-permute-start | bytes 6291464 | tf_op jit(solution)/shard_map/cond/branch_0_fun/ppermute | solution.py:332
  6.4 0.0 copy-start.4
  6.4 0.0 copy-start.8
  6.4 0.0 copy-start.12
  6.4 1.7 %slice_multiply_fusion = f32[2,1024,256]{2,1,0:T(8,128)S(1)} fusion(f32[2,1024,1024]{2,1,0:T(8,128)} %get-tuple-element.165.g_ref, f32[256]{0:T(256)S(1)} %slice.75), kind=kLoop, calls=%fused_computation | loop fusion | flops 524288 | bytes 4195328 | tf_op jit(solution)/shard_map/cond/branch_0_fun/mul | solution.py:331
  8.1 2.6 %collective-permute-start.3 = (f32[2,1024,256]{2,1,0:T(8,128)S(1)}, f32[2,1024,256]{2,1,0:T(8,128)S(1)}, u32[]{:S(2)}, u32[]{:S(2)}) collective-permute-start(f32[2,1024,256]{2,1,0:T(8,128)S(1)} %slice_multiply_fusion), channel_id=1, source_target_pairs={{1,0},{2,1},{3,2},{4,3},{5,4},{6,5},{7,6},{8,7},{9,8},{10,9},{11,1... | collective-permute-start | bytes 6291464 | tf_op jit(solution)/shard_map/cond/branch_0_fun/ppermute | solution.py:332
  10.7 0.0 copy-done
  10.7 0.0 copy-done.4
  10.8 0.0 copy-done.8
  10.8 0.0 copy-done.12
  10.8 19.7 %branch_0_fun.6 = (bf16[1024,2048]{1,0:T(8,128)(2,1)S(1)}, bf16[1024,2048]{1,0:T(8,128)(2,1)S(1)}, f32[23,128,128]{2,1,0:T(8,128)S(1)}, f32[10,128,128]{2,1,0:T(8,128)S(1)}, f32[11,128,128]{2,1,0:T(8,128)S(1)}) custom-call(s32[8]{0:T(128)S(1)} %copy-done.4, s32[4]{0:T(128)S(1)} %copy-done.12, f32[5,128]{1,0:T(8,128)S(1)} %copy-done.8, ...), custom_call_target="tpu_custom_call" | custom-call | flops 8053063680 | bytes 8388608 | tf_op jit(solution)/shard_map/cond/branch_0_fun/pallas_call | solution.py:131
  30.5 0.1 slice_multiply_fusion.2
  30.7 1.9 %collective-permute-start.5 = (f32[2,1024,128]{2,1,0:T(8,128)S(1)}, f32[2,1024,128]{2,1,0:T(8,128)S(1)}, u32[]{:S(2)}, u32[]{:S(2)}) collective-permute-start(f32[2,1024,128]{2,1,0:T(8,128)S(1)} %slice_multiply_fusion.2), channel_id=1, source_target_pairs={{1,0},{2,1},{3,2},{4,3},{5,4},{6,5},{7,6},{8,7},{9,8},{10,9},{11,1... | collective-permute-start | bytes 3145736 | tf_op jit(solution)/shard_map/cond/branch_0_fun/ppermute | solution.py:332
  32.6 0.6 collective-permute-start
  33.2 0.0 collective-permute-done.1.got
  33.2 3.5 %branch_0_fun.7 = (f32[2,128,128]{2,1,0:T(8,128)S(1)}, f32[8,128,128]{2,1,0:T(8,128)S(1)}, f32[8,128,128]{2,1,0:T(8,128)S(1)}) custom-call(f32[2,1024,256]{2,1,0:T(8,128)S(1)} %collective-permute-done.1.got, bf16[1024,2048]{1,0:T(8,128)(2,1)S(1)} %get-tuple-element.60.ah, bf16[1024,2048]{1,0:T(8,128)(2,1)S(1)} %get-tuple-element.61.al, ...), custom_call_target="tpu_custom_call" | custom-call | flops 2013265920 | bytes 2097152 | tf_op jit(solution)/shard_map/cond/branch_0_fun/pallas_call | solution.py:214
  36.7 1.5 %collective-permute-start.2 = (f32[8,128,128]{2,1,0:T(8,128)S(1)}, f32[8,128,128]{2,1,0:T(8,128)S(1)}, u32[]{:S(2)}, u32[]{:S(2)}) collective-permute-start(f32[8,128,128]{2,1,0:T(8,128)S(1)} %get-tuple-element.64), channel_id=1, source_target_pairs={{0,16},{16,0},{1,17},{17,1},{2,18},{18,2},{3,19},{19,3},{4,20},{20... | collective-permute-start | bytes 1572872 | tf_op jit(solution)/shard_map/cond/branch_0_fun/ppermute | solution.py:321
  38.2 14.1 %collective-permute-done.3.got = f32[2,1024,256]{2,1,0:T(8,128)S(1)} collective-permute-done((f32[2,1024,256]{2,1,0:T(8,128)S(1)}, f32[2,1024,256]{2,1,0:T(8,128)S(1)}, u32[]{:S(2)}, u32[]{:S(2)}) %collective-permute-start.3) | collective-permute-done | bytes 2097184 | tf_op jit(solution)/shard_map/cond/branch_0_fun/ppermute | solution.py:332
  52.3 2.4 %branch_0_fun.8 = (f32[6,128,128]{2,1,0:T(8,128)S(1)}, f32[6,128,128]{2,1,0:T(8,128)S(1)}) custom-call(f32[2,1024,256]{2,1,0:T(8,128)S(1)} %collective-permute-done.3.got, bf16[1024,2048]{1,0:T(8,128)(2,1)S(1)} %get-tuple-element.60.ah, bf16[1024,2048]{1,0:T(8,128)(2,1)S(1)} %get-tuple-element.61.al, f32[23,128,128]{2,1,0:T(8,128)S(1)} %get-tuple-element.55.refs_0_.own0), custom_call_target="tpu_custom_call" | custom-call | flops 1207959552 | bytes 2097152 | tf_op jit(solution)/shard_map/cond/branch_0_fun/pallas_call | solution.py:214
  54.8 0.6 collective-permute-start.4
  55.4 8.2 %collective-permute-done.5.got = f32[2,1024,128]{2,1,0:T(8,128)S(1)} collective-permute-done((f32[2,1024,128]{2,1,0:T(8,128)S(1)}, f32[2,1024,128]{2,1,0:T(8,128)S(1)}, u32[]{:S(2)}, u32[]{:S(2)}) %collective-permute-start.5) | collective-permute-done | bytes 1048608 | tf_op jit(solution)/shard_map/cond/branch_0_fun/ppermute | solution.py:332
  63.6 0.6 branch_0_fun.10.k1
  64.2 1.3 %collective-permute-start.6 = (f32[1,128,128]{2,1,0:T(8,128)S(1)}, f32[1,128,128]{2,1,0:T(8,128)S(1)}, u32[]{:S(2)}, u32[]{:S(2)}) collective-permute-start(f32[1,128,128]{2,1,0:T(8,128)S(1)} %branch_0_fun.10.k1), channel_id=1, source_target_pairs={{0,16},{1,17},{2,18},{3,19},{4,20},{5,21},{6,22},{7,23},{8,24},{9,... | collective-permute-start | bytes 196616 | tf_op jit(solution)/shard_map/cond/branch_0_fun/ppermute | solution.py:321
  65.5 0.0 collective-permute-done.swapped
  65.5 5.8 %collective-permute-done.4.refs_4_.c0 = f32[6,128,128]{2,1,0:T(8,128)S(1)} collective-permute-done((f32[6,128,128]{2,1,0:T(8,128)S(1)}, f32[6,128,128]{2,1,0:T(8,128)S(1)}, u32[]{:S(2)}, u32[]{:S(2)}) %collective-permute-start.4) | collective-permute-done | bytes 393248 | tf_op jit(solution)/shard_map/cond/branch_0_fun/ppermute | solution.py:321
  71.4 0.0 collective-permute-done.2.refs_2_
  71.4 5.3 %branch_0_fun.9.old = f32[512,1024]{1,0:T(8,128)} custom-call(s32[1]{0:T(128)} %get-tuple-element.48.window, f32[23,128,128]{2,1,0:T(8,128)S(1)} %get-tuple-element.55.refs_0_.own0, f32[10,128,128]{2,1,0:T(8,128)S(1)} %get-tuple-element.56.own1, f32[11,128,128]{2,1,0:T(8,128)S(1)} %collective-permute-done.swapped, ...), custom_call_target="tpu_custom_call" | custom-call | flops 1000000000 | bytes 12582912 | tf_op jit(solution)/shard_map/cond/branch_0_fun/pallas_call | solution.py:353
  76.7 0.0 collective-permute-done.6.c1
  76.7 2.4 %branch_0_fun.11 = f32[512,1024]{1,0:T(8,128)} custom-call(s32[1]{0:T(128)} %get-tuple-element.48.window, f32[512,1024]{1,0:T(8,128)} %branch_0_fun.9.old, f32[6,128,128]{2,1,0:T(8,128)S(1)} %get-tuple-element.65.refs_3_.k0, f32[1,128,128]{2,1,0:T(8,128)S(1)} %branch_0_fun.10.k1, ...), custom_call_target="tpu_custom_call", output_to_operand_aliasing={{}: (1, {})} | custom-call | flops 10000000 | bytes 393216 | tf_op jit(solution)/shard_map/cond/branch_0_fun/pallas_call | solution.py:355
  (3 shorter events, 0.0 us)
Async XLA Ops:
  1.4 9.3 %copy-start = (f32[2,1024,1024]{2,1,0:T(8,128)S(1)}, f32[2,1024,1024]{2,1,0:T(8,128)}, u32[]{:S(2)}) copy-start(f32[2,1024,1024]{2,1,0:T(8,128)} %get-tuple-element.165.g_ref) | copy-start | bytes 25165828 | tf_op jit(solution)/shard_map/cond
  3.3 29.9 %collective-permute-start.1 = (f32[2,1024,256]{2,1,0:T(8,128)S(1)}, f32[2,1024,256]{2,1,0:T(8,128)S(1)}, u32[]{:S(2)}, u32[]{:S(2)}) collective-permute-start(f32[2,1024,256]{2,1,0:T(8,128)S(1)} %slice_multiply_fusion.1), channel_id=1, source_target_pairs={{1,0},{2,1},{3,2},{4,3},{5,4},{6,5},{7,6},{8,7},{9,8},{10,9},{11,1... | collective-permute-start | bytes 6291464 | tf_op jit(solution)/shard_map/cond/branch_0_fun/ppermute | solution.py:332
  6.4 4.4 %copy-start.4 = (s32[8]{0:T(128)S(1)}, s32[8]{0:T(128)}, u32[]{:S(2)}) copy-start(s32[8]{0:T(128)} %get-tuple-element.153.counts) | copy-start | bytes 100 | tf_op jit(solution)/shard_map/cond
  6.4 4.4 %copy-start.8 = (f32[5,128]{1,0:T(8,128)S(1)}, f32[5,128]{1,0:T(8,128)}, u32[]{:S(2)}) copy-start(f32[5,128]{1,0:T(8,128)} %get-tuple-element.161.table) | copy-start | bytes 7684 | tf_op jit(solution)/shard_map/cond
  6.4 4.4 %copy-start.12 = (s32[4]{0:T(128)S(1)}, s32[4]{0:T(128)}, u32[]{:S(2)}) copy-start(s32[4]{0:T(128)} %get-tuple-element.157.pops) | copy-start | bytes 52 | tf_op jit(solution)/shard_map/cond
  8.1 44.2 %collective-permute-start.3 = (f32[2,1024,256]{2,1,0:T(8,128)S(1)}, f32[2,1024,256]{2,1,0:T(8,128)S(1)}, u32[]{:S(2)}, u32[]{:S(2)}) collective-permute-start(f32[2,1024,256]{2,1,0:T(8,128)S(1)} %slice_multiply_fusion), channel_id=1, source_target_pairs={{1,0},{2,1},{3,2},{4,3},{5,4},{6,5},{7,6},{8,7},{9,8},{10,9},{11,1... | collective-permute-start | bytes 6291464 | tf_op jit(solution)/shard_map/cond/branch_0_fun/ppermute | solution.py:332
  30.7 32.9 %collective-permute-start.5 = (f32[2,1024,128]{2,1,0:T(8,128)S(1)}, f32[2,1024,128]{2,1,0:T(8,128)S(1)}, u32[]{:S(2)}, u32[]{:S(2)}) collective-permute-start(f32[2,1024,128]{2,1,0:T(8,128)S(1)} %slice_multiply_fusion.2), channel_id=1, source_target_pairs={{1,0},{2,1},{3,2},{4,3},{5,4},{6,5},{7,6},{8,7},{9,8},{10,9},{11,1... | collective-permute-start | bytes 3145736 | tf_op jit(solution)/shard_map/cond/branch_0_fun/ppermute | solution.py:332
  32.6 32.9 %collective-permute-start = (f32[11,128,128]{2,1,0:T(8,128)S(1)}, f32[11,128,128]{2,1,0:T(8,128)S(1)}, u32[]{:S(2)}, u32[]{:S(2)}) collective-permute-start(f32[11,128,128]{2,1,0:T(8,128)S(1)} %get-tuple-element.59), channel_id=1, source_target_pairs={{0,16},{16,0},{1,17},{17,1},{2,18},{18,2},{3,19},{19,3},{4,20},{20... | collective-permute-start | bytes 2162696 | tf_op jit(solution)/shard_map/cond/branch_0_fun/ppermute | solution.py:321
  36.7 34.7 %collective-permute-start.2 = (f32[8,128,128]{2,1,0:T(8,128)S(1)}, f32[8,128,128]{2,1,0:T(8,128)S(1)}, u32[]{:S(2)}, u32[]{:S(2)}) collective-permute-start(f32[8,128,128]{2,1,0:T(8,128)S(1)} %get-tuple-element.64), channel_id=1, source_target_pairs={{0,16},{16,0},{1,17},{17,1},{2,18},{18,2},{3,19},{19,3},{4,20},{20... | collective-permute-start | bytes 1572872 | tf_op jit(solution)/shard_map/cond/branch_0_fun/ppermute | solution.py:321
  54.8 16.6 %collective-permute-start.4 = (f32[6,128,128]{2,1,0:T(8,128)S(1)}, f32[6,128,128]{2,1,0:T(8,128)S(1)}, u32[]{:S(2)}, u32[]{:S(2)}) collective-permute-start(f32[6,128,128]{2,1,0:T(8,128)S(1)} %get-tuple-element.66), channel_id=1, source_target_pairs={{0,16},{16,0},{1,17},{17,1},{2,18},{18,2},{3,19},{19,3},{4,20},{20... | collective-permute-start | bytes 1179656 | tf_op jit(solution)/shard_map/cond/branch_0_fun/ppermute | solution.py:321
  64.2 12.5 %collective-permute-start.6 = (f32[1,128,128]{2,1,0:T(8,128)S(1)}, f32[1,128,128]{2,1,0:T(8,128)S(1)}, u32[]{:S(2)}, u32[]{:S(2)}) collective-permute-start(f32[1,128,128]{2,1,0:T(8,128)S(1)} %branch_0_fun.10.k1), channel_id=1, source_target_pairs={{0,16},{1,17},{2,18},{3,19},{4,20},{5,21},{6,22},{7,23},{8,24},{9,... | collective-permute-start | bytes 196616 | tf_op jit(solution)/shard_map/cond/branch_0_fun/ppermute | solution.py:321

commit v2 on v1

--- a/solution.py
+++ b/solution.py
@@ -11,6 +11,7 @@
 WIN = 1024
 TILE = 128
 STRIP = 256
+OWN_STRIP = 1024
 F32 = jnp.float32
 BF16 = jnp.bfloat16
 SMEM = pl.BlockSpec(memory_space=pltpu.SMEM)
@@ -41,14 +42,16 @@
         for wide in HOPS[steps]:
             self.hops.append(Hop(tile, wide, steps, tiles))
             tile += wide
-        spare = sum(max(0, hop.bottom - hop.top) for hop in self.hops[:-1])
+        assert self.hops[-2].first >= self.half
+        spare = sum(max(0, hop.bottom - hop.top) for hop in self.hops[:-2])
         self.first_swap = max(self.n1, self.n0 - spare)
         left = self.first_swap
-        for hop in self.hops[:-1]:
+        for hop in self.hops[:-2]:
             take = max(0, min(self.n0 - left, hop.bottom - hop.top))
             hop.rest = (left, take)
             hop.swap = max(hop.bottom, hop.top + take)
             left += take
+        assert left == self.n0 or left == self.first_swap > self.n0
 
 
 def split(x):
@@ -80,16 +83,16 @@
         columns = slice(w * TILE, (w + 1) * TILE)
 
         def prepare(i, carry):
-            c, k = i // (people // STRIP), i % (people // STRIP)
-            deep = pl.ds(pl.multiple_of(i * STRIP, STRIP), STRIP)
-            x = g_ref[c, pl.ds(pl.multiple_of(k * STRIP, STRIP), STRIP), columns] * mask
+            c, k = i // (people // OWN_STRIP), i % (people // OWN_STRIP)
+            deep = pl.ds(pl.multiple_of(i * OWN_STRIP, OWN_STRIP), OWN_STRIP)
+            x = g_ref[c, pl.ds(pl.multiple_of(k * OWN_STRIP, OWN_STRIP), OWN_STRIP), columns] * mask
             high[deep, columns], low[deep, columns] = split(x)
             share = table[pops[group * cohorts + c], place]
             coef = jnp.full((1, TILE), share, F32) / jnp.full((1, TILE), total, F32) * (1.0 / people)
             ah[rows, deep], al[rows, deep] = split((x * coef).T)
             return carry
 
-        lax.fori_loop(0, cohorts * people // STRIP, prepare, 0)
+        lax.fori_loop(0, cohorts * people // OWN_STRIP, prepare, 0)
 
     def block(q, carry):
         rows = pl.ds(pl.multiple_of(q * span, span), span)
@@ -210,7 +213,7 @@
     deep = ah.shape[1]
     span = hop.wide * TILE
     args = [got, ah, al] + ([own0] if hop.rest[1] else [])
-    sizes = ([hop.top] if hop.top else []) + [hop.bottom] + ([hop.swap] if tag + 1 < len(plan.hops) else [])
+    sizes = ([hop.top] if hop.top else []) + [hop.bottom] + ([hop.swap] if tag + 2 < len(plan.hops) else [])
     outs = pl.pallas_call(
         functools.partial(hop_kernel, plan, hop),
         in_specs=[VMEM] * len(args),
@@ -229,20 +232,28 @@
     return top, outs[0], outs[-1]
 
 
-def skew(tile):
-    groups = [tile[g : g + 8] for g in range(0, TILE, 8)]
-    tile = jnp.concatenate([pltpu.roll(x, (TILE - 8 * g) % TILE, 1) if g else x for g, x in enumerate(groups)], axis=0)
-    row = lax.broadcasted_iota(jnp.int32, (TILE, TILE), 0)
+def skew(tiles, group):
+    rows = tiles[0].shape[0]
+    result = []
+    for tile in tiles:
+        parts = []
+        for g in range(rows // 8):
+            shift = (TILE - 8 * g - group * 8) % TILE
+            parts.append(pltpu.roll(tile[8 * g : 8 * g + 8], shift, 1))
+        result.append(jnp.concatenate(parts, axis=0))
+    row = lax.broadcasted_iota(jnp.int32, (rows, TILE), 0)
     for bit in (1, 2, 4):
-        tile = jnp.where((row & bit) != 0, pltpu.roll(tile, TILE - bit, 1), tile)
-    return tile
-
-
-def band_tile(this, after, step, window):
-    lane = lax.broadcasted_iota(jnp.int32, (TILE, TILE), 1)
-    row = lax.broadcasted_iota(jnp.int32, (TILE, TILE), 0)
-    mixed = jnp.where(lane + row < TILE, this, after)
-    return jnp.where(step * TILE + lane < window, mixed, 0.0)
+        odd = (row & bit) != 0
+        result = [jnp.where(odd, pltpu.roll(tile, TILE - bit, 1), tile) for tile in result]
+    return result
+
+
+def band_tiles(tiles, first, group, window):
+    shape = tiles[0].shape
+    lane = lax.broadcasted_iota(jnp.int32, shape, 1)
+    near = lane + lax.broadcasted_iota(jnp.int32, shape, 0) + group * 8 < TILE
+    for m, (this, after) in enumerate(zip(tiles, tiles[1:]), first):
+        yield jnp.where(m * TILE + lane < window, jnp.where(near, this, after), 0.0)
 
 
 def runs(plan, h, r, own, swapped, parts):
@@ -267,10 +278,9 @@
 
 def finish_kernel(plan, window, own0, own1, swapped, *refs):
     refs = list(refs)
-    band = refs.pop()
-    out = refs.pop()
+    sems, lines, band, edge, out = (refs.pop() for _ in range(5))
     parts = []
-    for hop in plan.hops[:-1]:
+    for hop in plan.hops[:-2]:
         top = refs.pop(0) if hop.top else None
         parts.append((top, refs.pop(0), refs.pop(0)))
     group = lax.axis_index("pop")
@@ -287,25 +297,66 @@
 
                     lax.fori_loop(0, count, add, 0)
 
-    def line(r, carry):
+    for i in range(edge.shape[0]):
+        row = plan.hops[-2].first + i
+        edge[i] = band[row - plan.half, plan.tiles + plan.hops[-2].tile - row - 1]
+
+    strip = 32
+    strips = TILE // strip
+
+    def line(i, carry):
+        r, q = i // strips, i % strips
+        inner = pl.ds(pl.multiple_of(q * strip, strip), strip)
+        rows = pl.ds(pl.multiple_of(i * strip, strip), strip)
+        tiles = skew([band[r, m, inner, :] for m in range(plan.steps + 1)], q * (strip // 8))
+        for m, tile in enumerate(band_tiles(tiles, 0, q * (strip // 8), window[0])):
+            lines[rows, m * TILE : (m + 1) * TILE] = tile
+        if plan.steps * TILE < out.shape[1]:
+            lines[rows, plan.steps * TILE :] = jnp.zeros((strip, out.shape[1] - plan.steps * TILE), F32)
+
+        @pl.when(q == strips - 1)
+        def _():
+            leave(r).start()
+
+        return carry
+
+    def leave(r):
         rows = pl.ds(pl.multiple_of(r * TILE, TILE), TILE)
-        this = skew(band[r, 0])
-        for m in range(plan.steps):
-            after = skew(band[r, m + 1])
-            out[rows, m * TILE : (m + 1) * TILE] = band_tile(this, after, m, window[0])
-            this = after
-        if plan.steps * TILE < out.shape[1]:
-            out[rows, plan.steps * TILE :] = jnp.zeros((TILE, out.shape[1] - plan.steps * TILE), F32)
-        return carry
-
-    lax.fori_loop(0, plan.half, line, 0)
-
-
-def last_kernel(plan, window, old, k0, k1, c0, c1, out):
-    this = skew(k0[k0.shape[0] - 1] + c0[plan.hops[-2].bottom - 1])
-    after = skew(k1[0] + c1[0])
-    fresh = band_tile(this, after, plan.steps - 1, window[0])
-    out[...] = jnp.where(lax.axis_index("pop") == 1, fresh, old[...])
+        return pltpu.make_async_copy(lines.at[rows, :], out.at[rows, :], sems.at[r])
+
+    lax.fori_loop(0, plan.half * strips, line, 0)
+    for r in range(plan.half):
+        leave(r).wait()
+
+
+def last_kernel(plan, window, old, edge, kept, came, kept_last, came_last, out, fresh, sems):
+    del old
+    hop, final = plan.hops[-2:]
+
+    @pl.when(lax.axis_index("pop") == 1)
+    def _():
+        copies = []
+        for i in range(edge.shape[0]):
+            row = hop.first + i
+            step = plan.tiles + hop.tile - row
+            tiles = [edge[i]]
+            for w in range(min(hop.wide, plan.steps + 1 - step)):
+                tiles.append(kept[i * hop.wide + w] + came[i * hop.wide + w])
+            if row >= final.first:
+                tiles.append(kept_last[row - final.first] + came_last[row - final.first])
+            for m, tile in enumerate(band_tiles(skew(tiles, 0), step - 1, 0, window[0])):
+                fresh[i, :, m * TILE : (m + 1) * TILE] = tile
+            width = (plan.steps - step + 1) * TILE
+            copies.append(
+                pltpu.make_async_copy(
+                    fresh.at[i, :, pl.ds(0, width)],
+                    out.at[pl.ds((row - plan.half) * TILE, TILE), pl.ds((step - 1) * TILE, width)],
+                    sems.at[i],
+                )
+            )
+            copies[-1].start()
+        for copy in copies:
+            copy.wait()
 
 
 def band(steps, genotypes, pop_id, window, tile_counts, weights):
@@ -320,48 +371,56 @@
     def swap(block, route):
         return lax.ppermute(block, "pop", route)
 
+    both = [(0, 1), (1, 0)]
     arrivals = []
     for j, hop in enumerate(plan.hops):
-        if j == 2:
-            ah, al, own0, own1, send = own_part(plan, genotypes, tile_counts, pop_id, weights)
-            valid, send, piece = lax.optimization_barrier((valid, send, piece))
-        elif j:
-            valid, piece = lax.optimization_barrier((valid, piece))
         span = slice(hop.tile * TILE, (hop.tile + hop.wide) * TILE)
         piece = genotypes[:, :, span] * valid[span]
         arrivals.append(lax.ppermute(piece, "snp", behind))
-    both = [(0, 1), (1, 0)]
-    swapped = swap(send, both)
+        if j == 0:
+            ah, al, own0, own1, send = own_part(plan, genotypes, tile_counts, pop_id, weights)
+            swapped = swap(send, both)
+            valid, send, piece = lax.optimization_barrier((valid, send, piece))
+        else:
+            valid, piece = lax.optimization_barrier((valid, piece))
     parts = []
     for j, (hop, got) in enumerate(zip(plan.hops, arrivals)):
         top, bottom, send = hop_part(plan, hop, got, ah, al, own0, j)
         route = both if hop.top or hop.rest[1] else both[:1]
         parts.append((top, bottom, swap(send, route)))
     lists = [own0, own1, swapped]
-    for part in parts[:-1]:
+    for part in parts[:-2]:
         lists += [x for x in part if x is not None]
     shape = jax.ShapeDtypeStruct((half * TILE, WIN), F32)
+    anywhere = pl.BlockSpec(memory_space=pl.ANY)
+    open_rows = tiles - plan.hops[-2].first
     finish = pl.pallas_call(
         functools.partial(finish_kernel, plan),
         in_specs=[SMEM] + [VMEM] * len(lists),
-        out_specs=VMEM,
-        out_shape=shape,
-        scratch_shapes=[pltpu.VMEM((half, steps + 1, TILE, TILE), F32)],
+        out_specs=[anywhere, VMEM],
+        out_shape=[shape, jax.ShapeDtypeStruct((open_rows, TILE, TILE), F32)],
+        scratch_shapes=[
+            pltpu.VMEM((half, steps + 1, TILE, TILE), F32),
+            pltpu.VMEM((half * TILE, WIN), F32),
+            pltpu.SemaphoreType.DMA((half,)),
+        ],
         cost_estimate=pl.CostEstimate(flops=10**9, bytes_accessed=6 * half * TILE * WIN * 4, transcendentals=0),
         compiler_params=PARAMS,
     )
-    out = finish(window, *lists)
-    corner = pl.BlockSpec((TILE, TILE), lambda i: (half - 1, steps - 1))
+    out, edge = finish(window, *lists)
     return pl.pallas_call(
         functools.partial(last_kernel, plan),
-        grid=(1,),
-        in_specs=[SMEM, corner, VMEM, VMEM, VMEM, VMEM],
-        out_specs=corner,
+        in_specs=[SMEM, anywhere] + [VMEM] * 5,
+        out_specs=anywhere,
         out_shape=shape,
         input_output_aliases={1: 0},
+        scratch_shapes=[
+            pltpu.VMEM((open_rows, TILE, (plan.hops[-2].wide + 1) * TILE), F32),
+            pltpu.SemaphoreType.DMA((open_rows,)),
+        ],
         cost_estimate=pl.CostEstimate(flops=10**7, bytes_accessed=6 * TILE * TILE * 4, transcendentals=0),
         compiler_params=PARAMS,
-    )(window, out, parts[-2][1], parts[-1][1], parts[-2][2], parts[-1][2])
+    )(window, out, edge, parts[-2][1], parts[-2][2], parts[-1][1], parts[-1][2])
 
 
 def solution(mesh):

time: 79.4 us -> 77.6 us (0.977)
  the two profiles are of different devices: /device:TPU:18 before, /device:TPU:1 now
where the time goes in v2:
time: 77.6 us; the launch traced here: 77.3 us
  Pallas kernels  29.9 us (39%)
  waiting for transfers between devices  24 us (31%)
  starting transfers between devices  16.4 us (21%)
  other arithmetic  5.52 us (7%)
  between operations  0.88 us (1%)
    ppermute x3, waiting for transfers between devices, band(): arrivals.append(lax.ppermute(piece, 'snp', behind))  24 us
    pallas_call x1, Pallas kernels, own_part(): pl.pallas_call(functools.partial(own_kernel, plan), grid=(snps // span,),...  16.1 us
    ppermute x4, starting transfers between devices, swap(): return lax.ppermute(block, 'pop', route)  10.6 us
    pallas_call x1, Pallas kernels, band(): out, edge = finish(window, *lists)  6.69 us
    pallas_call x3, Pallas kernels, hop_part(): pl.pallas_call(functools.partial(hop_kernel, plan, hop), in_specs=[VMEM]...  6.42 us
    ppermute x3, starting transfers between devices, band(): arrivals.append(lax.ppermute(piece, 'snp', behind))  5.77 us
    mul x4, other arithmetic, band(): piece = genotypes[:, :, span] * valid[span]  4.79 us
  transfers between devices with their start and end apart: 7, of which 3 were waited for; matrix products, arithmetic and copies ran while one was open for 4% of the time, Pallas kernels for 38%

profile of v2, /device:TPU:1, one launch (start us, length us, event | category | flops | bytes accessed | tf_op | source)
XLA Modules:
  0.0 77.3 jit_solution(10686632530148274837)
XLA Ops:
  0.7 76.4 %conditional.1 = (f32[512,1024]{1,0:T(8,128)}) conditional(s32[]{:T(128)} %clamp.3, (s32[8]{0:T(128)}, s32[4]{0:T(128)}, f32[5,128]{1,0:T(8,128)}, f32[2,1024,1024]{2,1,0:T(8,128)}, s32[1]{0:T(128)}) %tuple.29, (s32[8]{0:T(128)}, s32[4]{0:T(128)}, f32[5,128]{1,0:T(8,128)}, f32[2,1024,1024]{2,1,0:T(8,128)}, ...), branch_computations={%region_0.1_spmd, %region_1.2_spmd, %region_2.3_spmd, %region_3.4_... | conditional | flops 16916899840 | bytes 116026312 | solution.py:437
  0.7 0.7 convert_bitcast_fusion
  1.4 0.0 copy-start
  1.4 0.0 copy-start.4
  1.4 0.0 copy-start.8
  1.4 1.8 %slice_multiply_fusion.1 = f32[2,1024,256]{2,1,0:T(8,128)S(1)} fusion(f32[2,1024,1024]{2,1,0:T(8,128)} %get-tuple-element.161.g_ref, f32[256]{0:T(256)S(1)} %fusion), kind=kLoop, calls=%fused_computation.1 | loop fusion | flops 524288 | bytes 4195328 | tf_op jit(solution)/shard_map/cond/branch_0_fun/mul | solution.py:378
  3.2 1.9 %collective-permute-start.1 = (f32[2,1024,256]{2,1,0:T(8,128)S(1)}, f32[2,1024,256]{2,1,0:T(8,128)S(1)}, u32[]{:S(2)}, u32[]{:S(2)}) collective-permute-start(f32[2,1024,256]{2,1,0:T(8,128)S(1)} %slice_multiply_fusion.1), channel_id=1, source_target_pairs={{1,0},{2,1},{3,2},{4,3},{5,4},{6,5},{7,6},{8,7},{9,8},{10,9},{11,1... | collective-permute-start | bytes 6291464 | tf_op jit(solution)/shard_map/cond/branch_0_fun/ppermute | solution.py:379
  5.1 0.0 copy-done
  5.2 0.0 copy-done.4
  5.2 0.0 copy-done.8
  5.2 16.1 %branch_0_fun.6 = (bf16[1024,2048]{1,0:T(8,128)(2,1)S(1)}, bf16[1024,2048]{1,0:T(8,128)(2,1)S(1)}, f32[23,128,128]{2,1,0:T(8,128)S(1)}, f32[10,128,128]{2,1,0:T(8,128)S(1)}, f32[17,128,128]{2,1,0:T(8,128)S(1)}) custom-call(s32[8]{0:T(128)S(1)} %copy-done, s32[4]{0:T(128)S(1)} %copy-done.8, f32[5,128]{1,0:T(8,128)S(1)} %copy-done.4, ...), custom_call_target="tpu_custom_call" | custom-call | flops 8053063680 | bytes 8388608 | tf_op jit(solution)/shard_map/cond/branch_0_fun/pallas_call | solution.py:134
  21.3 1.7 %slice_multiply_fusion = f32[2,1024,256]{2,1,0:T(8,128)S(1)} fusion(f32[2,1024,1024]{2,1,0:T(8,128)} %get-tuple-element.161.g_ref, f32[256]{0:T(256)S(1)} %slice.75), kind=kLoop, calls=%fused_computation | loop fusion | flops 524288 | bytes 4195328 | tf_op jit(solution)/shard_map/cond/branch_0_fun/mul | solution.py:378
  23.0 1.9 %collective-permute-start.3 = (f32[2,1024,256]{2,1,0:T(8,128)S(1)}, f32[2,1024,256]{2,1,0:T(8,128)S(1)}, u32[]{:S(2)}, u32[]{:S(2)}) collective-permute-start(f32[2,1024,256]{2,1,0:T(8,128)S(1)} %slice_multiply_fusion), channel_id=1, source_target_pairs={{1,0},{2,1},{3,2},{4,3},{5,4},{6,5},{7,6},{8,7},{9,8},{10,9},{11,1... | collective-permute-start | bytes 6291464 | tf_op jit(solution)/shard_map/cond/branch_0_fun/ppermute | solution.py:379
  24.9 2.8 %collective-permute-start = (f32[17,128,128]{2,1,0:T(8,128)S(1)}, f32[17,128,128]{2,1,0:T(8,128)S(1)}, u32[]{:S(2)}, u32[]{:S(2)}) collective-permute-start(f32[17,128,128]{2,1,0:T(8,128)S(1)} %get-tuple-element.57), channel_id=1, source_target_pairs={{0,16},{16,0},{1,17},{17,1},{2,18},{18,2},{3,19},{19,3},{4,20},{20... | collective-permute-start | bytes 3342344 | tf_op jit(solution)/shard_map/cond/branch_0_fun/ppermute | solution.py:372
  27.7 1.3 %slice_multiply_fusion.2 = f32[2,1024,128]{2,1,0:T(8,128)S(1)} fusion(f32[2,1024,1024]{2,1,0:T(8,128)} %get-tuple-element.161.g_ref, f32[128]{0:T(128)S(1)} %slice.77), kind=kLoop, calls=%fused_computation.2 | loop fusion | flops 262144 | bytes 2097664 | tf_op jit(solution)/shard_map/cond/branch_0_fun/mul | solution.py:378
  29.0 1.9 %collective-permute-start.5 = (f32[2,1024,128]{2,1,0:T(8,128)S(1)}, f32[2,1024,128]{2,1,0:T(8,128)S(1)}, u32[]{:S(2)}, u32[]{:S(2)}) collective-permute-start(f32[2,1024,128]{2,1,0:T(8,128)S(1)} %slice_multiply_fusion.2), channel_id=1, source_target_pairs={{1,0},{2,1},{3,2},{4,3},{5,4},{6,5},{7,6},{8,7},{9,8},{10,9},{11,1... | collective-permute-start | bytes 3145736 | tf_op jit(solution)/shard_map/cond/branch_0_fun/ppermute | solution.py:379
  30.9 0.8 %collective-permute-done.1.got = f32[2,1024,256]{2,1,0:T(8,128)S(1)} collective-permute-done((f32[2,1024,256]{2,1,0:T(8,128)S(1)}, f32[2,1024,256]{2,1,0:T(8,128)S(1)}, u32[]{:S(2)}, u32[]{:S(2)}) %collective-permute-start.1) | collective-permute-done | bytes 2097184 | tf_op jit(solution)/shard_map/cond/branch_0_fun/ppermute | solution.py:379
  31.7 3.4 %branch_0_fun.7 = (f32[2,128,128]{2,1,0:T(8,128)S(1)}, f32[8,128,128]{2,1,0:T(8,128)S(1)}, f32[8,128,128]{2,1,0:T(8,128)S(1)}) custom-call(f32[2,1024,256]{2,1,0:T(8,128)S(1)} %collective-permute-done.1.got, bf16[1024,2048]{1,0:T(8,128)(2,1)S(1)} %get-tuple-element.58.ah, bf16[1024,2048]{1,0:T(8,128)(2,1)S(1)} %get-tuple-element.59.al, ...), custom_call_target="tpu_custom_call" | custom-call | flops 2013265920 | bytes 2097152 | tf_op jit(solution)/shard_map/cond/branch_0_fun/pallas_call | solution.py:217
  35.2 1.3 %collective-permute-start.2 = (f32[8,128,128]{2,1,0:T(8,128)S(1)}, f32[8,128,128]{2,1,0:T(8,128)S(1)}, u32[]{:S(2)}, u32[]{:S(2)}) collective-permute-start(f32[8,128,128]{2,1,0:T(8,128)S(1)} %get-tuple-element.62), channel_id=1, source_target_pairs={{0,16},{16,0},{1,17},{17,1},{2,18},{18,2},{3,19},{19,3},{4,20},{20... | collective-permute-start | bytes 1572872 | tf_op jit(solution)/shard_map/cond/branch_0_fun/ppermute | solution.py:372
  36.5 17.8 %collective-permute-done.3.got = f32[2,1024,256]{2,1,0:T(8,128)S(1)} collective-permute-done((f32[2,1024,256]{2,1,0:T(8,128)S(1)}, f32[2,1024,256]{2,1,0:T(8,128)S(1)}, u32[]{:S(2)}, u32[]{:S(2)}) %collective-permute-start.3) | collective-permute-done | bytes 2097184 | tf_op jit(solution)/shard_map/cond/branch_0_fun/ppermute | solution.py:379
  54.2 2.4 %branch_0_fun.9.kept = f32[6,128,128]{2,1,0:T(8,128)S(1)} custom-call(f32[2,1024,256]{2,1,0:T(8,128)S(1)} %collective-permute-done.3.got, bf16[1024,2048]{1,0:T(8,128)(2,1)S(1)} %get-tuple-element.58.ah, bf16[1024,2048]{1,0:T(8,128)(2,1)S(1)} %get-tuple-element.59.al), custom_call_target="tpu_custom_call" | custom-call | flops 1207959552 | bytes 2097152 | tf_op jit(solution)/shard_map/cond/branch_0_fun/pallas_call | solution.py:217
  56.6 3.1 %collective-permute-start.4 = (f32[6,128,128]{2,1,0:T(8,128)S(1)}, f32[6,128,128]{2,1,0:T(8,128)S(1)}, u32[]{:S(2)}, u32[]{:S(2)}) collective-permute-start(f32[6,128,128]{2,1,0:T(8,128)S(1)} %branch_0_fun.9.kept), channel_id=1, source_target_pairs={{0,16},{1,17},{2,18},{3,19},{4,20},{5,21},{6,22},{7,23},{8,24},{9,... | collective-permute-start | bytes 1179656 | tf_op jit(solution)/shard_map/cond/branch_0_fun/ppermute | solution.py:372
  59.7 5.4 %collective-permute-done.5.got = f32[2,1024,128]{2,1,0:T(8,128)S(1)} collective-permute-done((f32[2,1024,128]{2,1,0:T(8,128)S(1)}, f32[2,1024,128]{2,1,0:T(8,128)S(1)}, u32[]{:S(2)}, u32[]{:S(2)}) %collective-permute-start.5) | collective-permute-done | bytes 1048608 | tf_op jit(solution)/shard_map/cond/branch_0_fun/ppermute | solution.py:379
  65.2 0.6 branch_0_fun.10.kept_last
  65.8 3.4 %collective-permute-start.6 = (f32[1,128,128]{2,1,0:T(8,128)S(1)}, f32[1,128,128]{2,1,0:T(8,128)S(1)}, u32[]{:S(2)}, u32[]{:S(2)}) collective-permute-start(f32[1,128,128]{2,1,0:T(8,128)S(1)} %branch_0_fun.10.kept_last), channel_id=1, source_target_pairs={{0,16},{1,17},{2,18},{3,19},{4,20},{5,21},{6,22},{7,23},{8,24},{9,... | collective-permute-start | bytes 196616 | tf_op jit(solution)/shard_map/cond/branch_0_fun/ppermute | solution.py:372
  69.2 0.0 collective-permute-done.swapped
  69.2 0.0 collective-permute-done.2.refs_2_
  69.2 6.7 %branch_0_fun.8 = (f32[512,1024]{1,0:T(8,128)}, f32[3,128,128]{2,1,0:T(8,128)S(1)}) custom-call(s32[1]{0:T(128)} %get-tuple-element.48.window, f32[23,128,128]{2,1,0:T(8,128)S(1)} %get-tuple-element.55.refs_0_.own0, f32[10,128,128]{2,1,0:T(8,128)S(1)} %get-tuple-element.56.own1, f32[17,128,128]{2,1,0:T(8,128)S(1)} %collective-permute-done.swapped, ...), custom_call_target="tpu_custom_call" | custom-call | flops 1000000000 | bytes 12582912 | tf_op jit(solution)/shard_map/cond/branch_0_fun/pallas_call | solution.py:410
  75.9 0.0 collective-permute-done.6.came_last
  75.9 0.0 collective-permute-done.4.came
  75.9 0.7 branch_0_fun.11
  (3 shorter events, 0.0 us)
Async XLA Ops:
  1.4 3.7 %copy-start = (s32[8]{0:T(128)S(1)}, s32[8]{0:T(128)}, u32[]{:S(2)}) copy-start(s32[8]{0:T(128)} %get-tuple-element.149.counts) | copy-start | bytes 100 | tf_op jit(solution)/shard_map/cond
  1.4 3.7 %copy-start.4 = (f32[5,128]{1,0:T(8,128)S(1)}, f32[5,128]{1,0:T(8,128)}, u32[]{:S(2)}) copy-start(f32[5,128]{1,0:T(8,128)} %get-tuple-element.157.table) | copy-start | bytes 7684 | tf_op jit(solution)/shard_map/cond
  1.4 3.7 %copy-start.8 = (s32[4]{0:T(128)S(1)}, s32[4]{0:T(128)}, u32[]{:S(2)}) copy-start(s32[4]{0:T(128)} %get-tuple-element.153.pops) | copy-start | bytes 52 | tf_op jit(solution)/shard_map/cond
  3.2 28.5 %collective-permute-start.1 = (f32[2,1024,256]{2,1,0:T(8,128)S(1)}, f32[2,1024,256]{2,1,0:T(8,128)S(1)}, u32[]{:S(2)}, u32[]{:S(2)}) collective-permute-start(f32[2,1024,256]{2,1,0:T(8,128)S(1)} %slice_multiply_fusion.1), channel_id=1, source_target_pairs={{1,0},{2,1},{3,2},{4,3},{5,4},{6,5},{7,6},{8,7},{9,8},{10,9},{11,1... | collective-permute-start | bytes 6291464 | tf_op jit(solution)/shard_map/cond/branch_0_fun/ppermute | solution.py:379
  23.0 31.2 %collective-permute-start.3 = (f32[2,1024,256]{2,1,0:T(8,128)S(1)}, f32[2,1024,256]{2,1,0:T(8,128)S(1)}, u32[]{:S(2)}, u32[]{:S(2)}) collective-permute-start(f32[2,1024,256]{2,1,0:T(8,128)S(1)} %slice_multiply_fusion), channel_id=1, source_target_pairs={{1,0},{2,1},{3,2},{4,3},{5,4},{6,5},{7,6},{8,7},{9,8},{10,9},{11,1... | collective-permute-start | bytes 6291464 | tf_op jit(solution)/shard_map/cond/branch_0_fun/ppermute | solution.py:379
  24.9 44.3 %collective-permute-start = (f32[17,128,128]{2,1,0:T(8,128)S(1)}, f32[17,128,128]{2,1,0:T(8,128)S(1)}, u32[]{:S(2)}, u32[]{:S(2)}) collective-permute-start(f32[17,128,128]{2,1,0:T(8,128)S(1)} %get-tuple-element.57), channel_id=1, source_target_pairs={{0,16},{16,0},{1,17},{17,1},{2,18},{18,2},{3,19},{19,3},{4,20},{20... | collective-permute-start | bytes 3342344 | tf_op jit(solution)/shard_map/cond/branch_0_fun/ppermute | solution.py:372
  29.0 36.1 %collective-permute-start.5 = (f32[2,1024,128]{2,1,0:T(8,128)S(1)}, f32[2,1024,128]{2,1,0:T(8,128)S(1)}, u32[]{:S(2)}, u32[]{:S(2)}) collective-permute-start(f32[2,1024,128]{2,1,0:T(8,128)S(1)} %slice_multiply_fusion.2), channel_id=1, source_target_pairs={{1,0},{2,1},{3,2},{4,3},{5,4},{6,5},{7,6},{8,7},{9,8},{10,9},{11,1... | collective-permute-start | bytes 3145736 | tf_op jit(solution)/shard_map/cond/branch_0_fun/ppermute | solution.py:379
  35.2 34.0 %collective-permute-start.2 = (f32[8,128,128]{2,1,0:T(8,128)S(1)}, f32[8,128,128]{2,1,0:T(8,128)S(1)}, u32[]{:S(2)}, u32[]{:S(2)}) collective-permute-start(f32[8,128,128]{2,1,0:T(8,128)S(1)} %get-tuple-element.62), channel_id=1, source_target_pairs={{0,16},{16,0},{1,17},{17,1},{2,18},{18,2},{3,19},{19,3},{4,20},{20... | collective-permute-start | bytes 1572872 | tf_op jit(solution)/shard_map/cond/branch_0_fun/ppermute | solution.py:372
  56.6 19.3 %collective-permute-start.4 = (f32[6,128,128]{2,1,0:T(8,128)S(1)}, f32[6,128,128]{2,1,0:T(8,128)S(1)}, u32[]{:S(2)}, u32[]{:S(2)}) collective-permute-start(f32[6,128,128]{2,1,0:T(8,128)S(1)} %branch_0_fun.9.kept), channel_id=1, source_target_pairs={{0,16},{1,17},{2,18},{3,19},{4,20},{5,21},{6,22},{7,23},{8,24},{9,... | collective-permute-start | bytes 1179656 | tf_op jit(solution)/shard_map/cond/branch_0_fun/ppermute | solution.py:372
  65.8 10.1 %collective-permute-start.6 = (f32[1,128,128]{2,1,0:T(8,128)S(1)}, f32[1,128,128]{2,1,0:T(8,128)S(1)}, u32[]{:S(2)}, u32[]{:S(2)}) collective-permute-start(f32[1,128,128]{2,1,0:T(8,128)S(1)} %branch_0_fun.10.kept_last), channel_id=1, source_target_pairs={{0,16},{1,17},{2,18},{3,19},{4,20},{5,21},{6,22},{7,23},{8,24},{9,... | collective-permute-start | bytes 196616 | tf_op jit(solution)/shard_map/cond/branch_0_fun/ppermute | solution.py:372

commit v3 on v2

--- a/solution.py
+++ b/solution.py
@@ -11,7 +11,7 @@
 WIN = 1024
 TILE = 128
 STRIP = 256
-OWN_STRIP = 1024
+OWN_STRIP = 512
 F32 = jnp.float32
 BF16 = jnp.bfloat16
 SMEM = pl.BlockSpec(memory_space=pltpu.SMEM)
@@ -43,8 +43,11 @@
             self.hops.append(Hop(tile, wide, steps, tiles))
             tile += wide
         assert self.hops[-2].first >= self.half
+        assert self.hops[-1].first == tiles - 1 and self.hops[-1].wide == 1
         spare = sum(max(0, hop.bottom - hop.top) for hop in self.hops[:-2])
         self.first_swap = max(self.n1, self.n0 - spare)
+        self.even = self.n1 if steps == min(HOPS) else self.first_swap
+        self.extra = self.first_swap - self.even
         left = self.first_swap
         for hop in self.hops[:-2]:
             take = max(0, min(self.n0 - left, hop.bottom - hop.top))
@@ -66,7 +69,52 @@
     return result
 
 
-def own_kernel(plan, counts, pops, table, g_ref, ah, al, own0, own1, send, high, low):
+def piece_kernel(counts_ref, g_ref, out, counts, sems):
+    cohorts, people, span = out.shape
+    parts = (sems.shape[0] - 1) // cohorts
+    rows = people // parts
+    copies = []
+    for i in range(cohorts * parts):
+        c, k = i // parts, i % parts
+        area = (c, pl.ds(k * rows, rows))
+        copies.append(
+            pltpu.make_async_copy(g_ref.at[area + (pl.ds(0, span),)], out.at[area], sems.at[i])
+        )
+        copies[-1].start()
+    table = pltpu.make_async_copy(counts_ref, counts, sems.at[cohorts * parts])
+    table.start()
+    table.wait()
+    lane = lax.broadcasted_iota(jnp.int32, (1, TILE), 1)
+    mask = jnp.concatenate([(lane < counts[w]).astype(F32) for w in range(span // TILE)], axis=1)
+    for i, copy in enumerate(copies):
+        copy.wait()
+        c, k = i // parts, i % parts
+
+        def cut(j, carry, c=c, k=k):
+            area = pl.ds(pl.multiple_of(k * rows + j * 128, 128), 128)
+            out[c, area, :] = out[c, area, :] * mask
+            return carry
+
+        lax.fori_loop(0, rows // 128, cut, 0)
+
+
+def piece_part(genotypes, tile_counts, wide):
+    cohorts, people, _ = genotypes.shape
+    return pl.pallas_call(
+        piece_kernel,
+        in_specs=[pl.BlockSpec(memory_space=pl.ANY)] * 2,
+        out_specs=VMEM,
+        out_shape=jax.ShapeDtypeStruct((cohorts, people, wide * TILE), F32),
+        scratch_shapes=[pltpu.SMEM(tile_counts.shape, jnp.int32), pltpu.SemaphoreType.DMA((cohorts * 4 + 1,))],
+        cost_estimate=pl.CostEstimate(flops=10**6, bytes_accessed=8 * cohorts * people * wide * TILE, transcendentals=0),
+        compiler_params=PARAMS,
+        name="piece",
+    )(tile_counts, genotypes)
+
+
+def own_kernel(plan, counts, pops, table, g_ref, ah, al, own0, own1, send, *refs):
+    more = refs[0] if plan.extra else None
+    high, low = refs[-2:]
     cohorts, people, span = g_ref.shape
     wide = span // TILE
     step = pl.program_id(0)
@@ -116,9 +164,17 @@
                 def _():
                     own1[spot] = tile
 
-                @pl.when(inside & ((row < plan.half) == (group == 1)) & (spot < plan.first_swap))
+                other = inside & ((row < plan.half) == (group == 1))
+
+                @pl.when(other & (spot < plan.even))
                 def _():
                     send[spot] = tile
+
+                if more is not None:
+
+                    @pl.when(other & (spot >= plan.even) & (spot < plan.first_swap))
+                    def _():
+                        more[spot - plan.even] = tile
 
         return carry
 
@@ -130,12 +186,12 @@
     deep = cohorts * people
     span = 2 * TILE
     tall = jax.ShapeDtypeStruct((snps, deep), BF16)
-    sizes = (plan.n0, plan.n1, plan.first_swap)
+    sizes = [plan.n0, plan.n1, plan.even] + ([plan.extra] if plan.extra else [])
     return pl.pallas_call(
         functools.partial(own_kernel, plan),
         grid=(snps // span,),
         in_specs=[SMEM, SMEM, SMEM, pl.BlockSpec((cohorts, people, span), lambda t: (0, 0, t))],
-        out_specs=[VMEM] * 5,
+        out_specs=[VMEM] * (2 + len(sizes)),
         out_shape=[tall, tall] + [jax.ShapeDtypeStruct((n, TILE, TILE), F32) for n in sizes],
         scratch_shapes=[pltpu.VMEM((deep, span), BF16), pltpu.VMEM((deep, span), BF16)],
         cost_estimate=pl.CostEstimate(
@@ -234,15 +290,18 @@
 
 def skew(tiles, group):
     rows = tiles[0].shape[0]
+    low = lax.broadcasted_iota(jnp.int32, (8, TILE), 0)
+    row = lax.broadcasted_iota(jnp.int32, (rows, TILE), 0)
     result = []
     for tile in tiles:
         parts = []
         for g in range(rows // 8):
-            shift = (TILE - 8 * g - group * 8) % TILE
-            parts.append(pltpu.roll(tile[8 * g : 8 * g + 8], shift, 1))
+            part = tile[8 * g : 8 * g + 8]
+            shift = 2 * TILE - 8 * g - group * 8
+            near, far = pltpu.roll(part, shift % TILE, 1), pltpu.roll(part, (shift - 4) % TILE, 1)
+            parts.append(jnp.where(low >= 4, far, near))
         result.append(jnp.concatenate(parts, axis=0))
-    row = lax.broadcasted_iota(jnp.int32, (rows, TILE), 0)
-    for bit in (1, 2, 4):
+    for bit in (1, 2):
         odd = (row & bit) != 0
         result = [jnp.where(odd, pltpu.roll(tile, TILE - bit, 1), tile) for tile in result]
     return result
@@ -260,8 +319,9 @@
     row = h * plan.half + r
     start, count = plan.starts[row], plan.counts[row]
     result = []
-    edges = [(swapped, 0, plan.first_swap, 0)]
+    edges = [(swapped[0], 0, plan.even, 0)]
     if h == 0:
+        edges += [(more, plan.even, plan.extra, 0) for more in swapped[1:]]
         edges += [(part[2], hop.rest[0], hop.rest[1], hop.top) for hop, part in zip(plan.hops, parts)]
     for came, begin, length, base in edges:
         lo, hi = max(start, begin), min(start + count, begin + length)
@@ -276,8 +336,9 @@
     return result
 
 
-def finish_kernel(plan, window, own0, own1, swapped, *refs):
+def finish_kernel(plan, window, own0, own1, *refs):
     refs = list(refs)
+    swapped = [refs.pop(0) for _ in range(2 if plan.extra else 1)]
     sems, lines, band, edge, out = (refs.pop() for _ in range(5))
     parts = []
     for hop in plan.hops[:-2]:
@@ -301,7 +362,7 @@
         row = plan.hops[-2].first + i
         edge[i] = band[row - plan.half, plan.tiles + plan.hops[-2].tile - row - 1]
 
-    strip = 32
+    strip = 64
     strips = TILE // strip
 
     def line(i, carry):
@@ -313,25 +374,21 @@
             lines[rows, m * TILE : (m + 1) * TILE] = tile
         if plan.steps * TILE < out.shape[1]:
             lines[rows, plan.steps * TILE :] = jnp.zeros((strip, out.shape[1] - plan.steps * TILE), F32)
-
-        @pl.when(q == strips - 1)
-        def _():
-            leave(r).start()
-
+        leave(i).start()
         return carry
 
-    def leave(r):
-        rows = pl.ds(pl.multiple_of(r * TILE, TILE), TILE)
-        return pltpu.make_async_copy(lines.at[rows, :], out.at[rows, :], sems.at[r])
+    def leave(i):
+        rows = pl.ds(pl.multiple_of(i * strip, strip), strip)
+        return pltpu.make_async_copy(lines.at[rows, :], out.at[rows, :], sems.at[i])
 
     lax.fori_loop(0, plan.half * strips, line, 0)
-    for r in range(plan.half):
-        leave(r).wait()
-
-
-def last_kernel(plan, window, old, edge, kept, came, kept_last, came_last, out, fresh, sems):
+    for i in range(plan.half * strips):
+        leave(i).wait()
+
+
+def next_kernel(plan, window, old, edge, kept, came, out, ready, fresh, sems):
     del old
-    hop, final = plan.hops[-2:]
+    hop = plan.hops[-2]
 
     @pl.when(lax.axis_index("pop") == 1)
     def _():
@@ -342,11 +399,10 @@
             tiles = [edge[i]]
             for w in range(min(hop.wide, plan.steps + 1 - step)):
                 tiles.append(kept[i * hop.wide + w] + came[i * hop.wide + w])
-            if row >= final.first:
-                tiles.append(kept_last[row - final.first] + came_last[row - final.first])
-            for m, tile in enumerate(band_tiles(skew(tiles, 0), step - 1, 0, window[0])):
+            tiles = skew(tiles, 0)
+            for m, tile in enumerate(band_tiles(tiles, step - 1, 0, window[0])):
                 fresh[i, :, m * TILE : (m + 1) * TILE] = tile
-            width = (plan.steps - step + 1) * TILE
+            width = (len(tiles) - 1) * TILE
             copies.append(
                 pltpu.make_async_copy(
                     fresh.at[i, :, pl.ds(0, width)],
@@ -355,8 +411,22 @@
                 )
             )
             copies[-1].start()
+        ready[0] = tiles[-1]
         for copy in copies:
             copy.wait()
+
+
+def last_kernel(plan, window, old, ready, kept, came, out, fresh, sem):
+    del old
+
+    @pl.when(lax.axis_index("pop") == 1)
+    def _():
+        tiles = [ready[0]] + skew([kept[0] + came[0]], 0)
+        (fresh[...],) = band_tiles(tiles, plan.steps - 1, 0, window[0])
+        corner = out.at[pl.ds((plan.half - 1) * TILE, TILE), pl.ds((plan.steps - 1) * TILE, TILE)]
+        copy = pltpu.make_async_copy(fresh, corner, sem)
+        copy.start()
+        copy.wait()
 
 
 def band(steps, genotypes, pop_id, window, tile_counts, weights):
@@ -365,7 +435,6 @@
     half = tiles // 2
     assert snps == WIN and tiles % 2 == 0 and lax.axis_size("pop") == 2
     plan = Plan(steps, tiles)
-    valid = (tile_counts[:, None] > jnp.arange(TILE, dtype=jnp.int32)[None, :]).astype(F32).reshape(snps)
     behind = [(i + 1, i) for i in range(lax.axis_size("snp") - 1)]
 
     def swap(block, route):
@@ -375,12 +444,16 @@
     arrivals = []
     for j, hop in enumerate(plan.hops):
         span = slice(hop.tile * TILE, (hop.tile + hop.wide) * TILE)
-        piece = genotypes[:, :, span] * valid[span]
+        if j == 0:
+            piece = piece_part(genotypes, tile_counts, hop.wide)
+        else:
+            piece = genotypes[:, :, span] * valid[span]
         arrivals.append(lax.ppermute(piece, "snp", behind))
         if j == 0:
-            ah, al, own0, own1, send = own_part(plan, genotypes, tile_counts, pop_id, weights)
-            swapped = swap(send, both)
-            valid, send, piece = lax.optimization_barrier((valid, send, piece))
+            ah, al, own0, own1, send, *more = own_part(plan, genotypes, tile_counts, pop_id, weights)
+            swapped = [swap(send, both)] + [swap(x, both[1:]) for x in more]
+            counts, send, piece = lax.optimization_barrier((tile_counts, send, piece))
+            valid = (counts[:, None] > jnp.arange(TILE, dtype=jnp.int32)[None, :]).astype(F32).reshape(snps)
         else:
             valid, piece = lax.optimization_barrier((valid, piece))
     parts = []
@@ -388,7 +461,7 @@
         top, bottom, send = hop_part(plan, hop, got, ah, al, own0, j)
         route = both if hop.top or hop.rest[1] else both[:1]
         parts.append((top, bottom, swap(send, route)))
-    lists = [own0, own1, swapped]
+    lists = [own0, own1, *swapped]
     for part in parts[:-2]:
         lists += [x for x in part if x is not None]
     shape = jax.ShapeDtypeStruct((half * TILE, WIN), F32)
@@ -402,25 +475,37 @@
         scratch_shapes=[
             pltpu.VMEM((half, steps + 1, TILE, TILE), F32),
             pltpu.VMEM((half * TILE, WIN), F32),
-            pltpu.SemaphoreType.DMA((half,)),
+            pltpu.SemaphoreType.DMA((2 * half,)),
         ],
         cost_estimate=pl.CostEstimate(flops=10**9, bytes_accessed=6 * half * TILE * WIN * 4, transcendentals=0),
         compiler_params=PARAMS,
     )
     out, edge = finish(window, *lists)
+    tile = jax.ShapeDtypeStruct((1, TILE, TILE), F32)
+    cost = pl.CostEstimate(flops=10**7, bytes_accessed=6 * TILE * TILE * 4, transcendentals=0)
+    out, ready = pl.pallas_call(
+        functools.partial(next_kernel, plan),
+        in_specs=[SMEM, anywhere] + [VMEM] * 3,
+        out_specs=[anywhere, VMEM],
+        out_shape=[shape, tile],
+        input_output_aliases={1: 0},
+        scratch_shapes=[
+            pltpu.VMEM((open_rows, TILE, plan.hops[-2].wide * TILE), F32),
+            pltpu.SemaphoreType.DMA((open_rows,)),
+        ],
+        cost_estimate=cost,
+        compiler_params=PARAMS,
+    )(window, out, edge, parts[-2][1], parts[-2][2])
     return pl.pallas_call(
         functools.partial(last_kernel, plan),
-        in_specs=[SMEM, anywhere] + [VMEM] * 5,
+        in_specs=[SMEM, anywhere] + [VMEM] * 3,
         out_specs=anywhere,
         out_shape=shape,
         input_output_aliases={1: 0},
-        scratch_shapes=[
-            pltpu.VMEM((open_rows, TILE, (plan.hops[-2].wide + 1) * TILE), F32),
-            pltpu.SemaphoreType.DMA((open_rows,)),
-        ],
-        cost_estimate=pl.CostEstimate(flops=10**7, bytes_accessed=6 * TILE * TILE * 4, transcendentals=0),
+        scratch_shapes=[pltpu.VMEM((TILE, TILE), F32), pltpu.SemaphoreType.DMA],
+        cost_estimate=cost,
         compiler_params=PARAMS,
-    )(window, out, edge, parts[-2][1], parts[-2][2], parts[-1][1], parts[-1][2])
+    )(window, out, ready, parts[-1][1], parts[-1][2])
 
 
 def solution(mesh):

time: 77.6 us -> 75.6 us (0.974)
  the two profiles are of different devices: /device:TPU:1 before, /device:TPU:7 now
where the time goes in v3:
time: 75.6 us; the launch traced here: 75.3 us
  Pallas kernels  33.3 us (44%)
  waiting for transfers between devices  26.4 us (35%)
  starting transfers between devices  13.4 us (18%)
  between operations  0.9 us (1%)
  loops' own time  0.79 us (1%)
    ppermute x3, waiting for transfers between devices, band(): arrivals.append(lax.ppermute(piece, 'snp', behind))  26.4 us
    pallas_call x1, Pallas kernels, own_part(): pl.pallas_call(functools.partial(own_kernel, plan), grid=(snps // span,),...  17.3 us
    ppermute x3, starting transfers between devices, band(): arrivals.append(lax.ppermute(piece, 'snp', behind))  7.28 us
    pallas_call x3, Pallas kernels, hop_part(): pl.pallas_call(functools.partial(hop_kernel, plan, hop), in_specs=[VMEM]...  6.42 us
    ppermute x5, starting transfers between devices, swap(): return lax.ppermute(block, 'pop', route)  6.11 us
    pallas_call x1, Pallas kernels, band(): out, edge = finish(window, *lists)  4.24 us
    pallas_call x1, Pallas kernels, band(): pl.pallas_call(functools.partial(next_kernel, plan), in_specs=[SMEM, anyw...  2.07 us
    pallas_call x1, Pallas kernels, piece_part(): pl.pallas_call(piece_kernel, in_specs=[pl.BlockSpec(memory_space=pl.ANY)]...  1.77 us
  transfers between devices with their start and end apart: 8, of which 3 were waited for; matrix products, arithmetic and copies ran while one was open for 1% of the time, Pallas kernels for 40%

profile of v3, /device:TPU:7, one launch (start us, length us, event | category | flops | bytes accessed | tf_op | source)
XLA Modules:
  0.0 75.3 jit_solution(15209890739878954623)
XLA Ops:
  0.7 74.4 %conditional.1 = (f32[512,1024]{1,0:T(8,128)}) conditional(s32[]{:T(128)} %clamp.3, (s32[8]{0:T(128)}, s32[4]{0:T(128)}, f32[5,128]{1,0:T(8,128)}, f32[2,1024,1024]{2,1,0:T(8,128)}, s32[1]{0:T(128)}) %tuple.29, (s32[8]{0:T(128)}, s32[4]{0:T(128)}, f32[5,128]{1,0:T(8,128)}, f32[2,1024,1024]{2,1,0:T(8,128)}, ...), branch_computations={%region_0.1_spmd, %region_1.2_spmd, %region_2.3_spmd, %region_3.4_... | conditional | flops 16927375360 | bytes 124805136 | solution.py:522
  0.7 0.0 copy-start
  0.7 0.0 copy-start.4
  0.7 0.0 copy-start.8
  0.7 0.0 copy-start.12
  0.7 1.8 %piece.4 = f32[2,1024,256]{2,1,0:T(8,128)S(1)} custom-call(s32[8]{0:T(128)} %get-tuple-element.66.counts.counts_ref, f32[2,1024,1024]{2,1,0:T(8,128)} %get-tuple-element.170.g_ref), custom_call_target="tpu_custom_call" | custom-call | flops 1000000 | bytes 4194304 | tf_op jit(solution)/shard_map/cond/branch_0_fun/piece/pallas_call | solution.py:103
  2.5 2.8 %collective-permute-start.2 = (f32[2,1024,256]{2,1,0:T(8,128)S(1)}, f32[2,1024,256]{2,1,0:T(8,128)S(1)}, u32[]{:S(2)}, u32[]{:S(2)}) collective-permute-start(f32[2,1024,256]{2,1,0:T(8,128)S(1)} %piece.4), channel_id=1, source_target_pairs={{1,0},{2,1},{3,2},{4,3},{5,4},{6,5},{7,6},{8,7},{9,8},{10,9},{11,1... | collective-permute-start | bytes 6291464 | tf_op jit(solution)/shard_map/cond/branch_0_fun/ppermute | solution.py:451
  5.4 0.0 copy-done
  5.4 0.0 copy-done.4
  5.4 0.0 copy-done.8
  5.4 0.0 copy-done.12
  5.4 17.3 %branch_0_fun.7 = (bf16[1024,2048]{1,0:T(8,128)(2,1)S(1)}, bf16[1024,2048]{1,0:T(8,128)(2,1)S(1)}, f32[23,128,128]{2,1,0:T(8,128)S(1)}, f32[10,128,128]{2,1,0:T(...) custom-call(s32[8]{0:T(128)S(1)} %copy-done.4, s32[4]{0:T(128)S(1)} %copy-done.12, ...), custom_call_target="tpu_custom_call" | custom-call | flops 8053063680 | bytes 8388608 | tf_op jit(solution)/shard_map/cond/branch_0_fun/pallas_call | solution.py:190
  22.7 0.1 convert_bitcast_fusion
  22.8 0.3 slice_multiply_fusion
  23.1 1.9 %collective-permute-start.4 = (f32[2,1024,256]{2,1,0:T(8,128)S(1)}, f32[2,1024,256]{2,1,0:T(8,128)S(1)}, u32[]{:S(2)}, u32[]{:S(2)}) collective-permute-start(f32[2,1024,256]{2,1,0:T(8,128)S(1)} %slice_multiply_fusion), channel_id=1, source_target_pairs={{1,0},{2,1},{3,2},{4,3},{5,4},{6,5},{7,6},{8,7},{9,8},{10,9},{11,1... | collective-permute-start | bytes 6291464 | tf_op jit(solution)/shard_map/cond/branch_0_fun/ppermute | solution.py:451
  25.0 0.1 slice_multiply_fusion.1
  25.2 2.5 %collective-permute-start.6 = (f32[2,1024,128]{2,1,0:T(8,128)S(1)}, f32[2,1024,128]{2,1,0:T(8,128)S(1)}, u32[]{:S(2)}, u32[]{:S(2)}) collective-permute-start(f32[2,1024,128]{2,1,0:T(8,128)S(1)} %slice_multiply_fusion.1), channel_id=1, source_target_pairs={{1,0},{2,1},{3,2},{4,3},{5,4},{6,5},{7,6},{8,7},{9,8},{10,9},{11,1... | collective-permute-start | bytes 3145736 | tf_op jit(solution)/shard_map/cond/branch_0_fun/ppermute | solution.py:451
  27.7 0.1 collective-permute-start
  27.8 3.2 %collective-permute-done.2.got = f32[2,1024,256]{2,1,0:T(8,128)S(1)} collective-permute-done((f32[2,1024,256]{2,1,0:T(8,128)S(1)}, f32[2,1024,256]{2,1,0:T(8,128)S(1)}, u32[]{:S(2)}, u32[]{:S(2)}) %collective-permute-start.2) | collective-permute-done | bytes 2097184 | tf_op jit(solution)/shard_map/cond/branch_0_fun/ppermute | solution.py:451
  31.0 3.4 %branch_0_fun.8 = (f32[2,128,128]{2,1,0:T(8,128)S(1)}, f32[8,128,128]{2,1,0:T(8,128)S(1)}, f32[8,128,128]{2,1,0:T(8,128)S(1)}) custom-call(f32[2,1024,256]{2,1,0:T(8,128)S(1)} %collective-permute-done.2.got, bf16[1024,2048]{1,0:T(8,128)(2,1)S(1)} %get-tuple-element.59.ah, bf16[1024,2048]{1,0:T(8,128)(2,1)S(1)} %get-tuple-element.60.al, ...), custom_call_target="tpu_custom_call" | custom-call | flops 2013265920 | bytes 2097152 | tf_op jit(solution)/shard_map/cond/branch_0_fun/pallas_call | solution.py:273
  34.5 0.3 collective-permute-start.3
  34.8 3.1 %collective-permute-start.1 = (f32[7,128,128]{2,1,0:T(8,128)S(1)}, f32[7,128,128]{2,1,0:T(8,128)S(1)}, u32[]{:S(2)}, u32[]{:S(2)}) collective-permute-start(f32[7,128,128]{2,1,0:T(8,128)S(1)} %get-tuple-element.58), channel_id=1, source_target_pairs={{16,0},{17,1},{18,2},{19,3},{20,4},{21,5},{22,6},{23,7},{24,8},{25... | collective-permute-start | bytes 1376264 | tf_op jit(solution)/shard_map/cond/branch_0_fun/ppermute | solution.py:441
  37.9 15.6 %collective-permute-done.4.got = f32[2,1024,256]{2,1,0:T(8,128)S(1)} collective-permute-done((f32[2,1024,256]{2,1,0:T(8,128)S(1)}, f32[2,1024,256]{2,1,0:T(8,128)S(1)}, u32[]{:S(2)}, u32[]{:S(2)}) %collective-permute-start.4) | collective-permute-done | bytes 2097184 | tf_op jit(solution)/shard_map/cond/branch_0_fun/ppermute | solution.py:451
  53.5 2.4 %branch_0_fun.10.kept = f32[6,128,128]{2,1,0:T(8,128)S(1)} custom-call(f32[2,1024,256]{2,1,0:T(8,128)S(1)} %collective-permute-done.4.got, bf16[1024,2048]{1,0:T(8,128)(2,1)S(1)} %get-tuple-element.59.ah, bf16[1024,2048]{1,0:T(8,128)(2,1)S(1)} %get-tuple-element.60.al), custom_call_target="tpu_custom_call" | custom-call | flops 1207959552 | bytes 2097152 | tf_op jit(solution)/shard_map/cond/branch_0_fun/pallas_call | solution.py:273
  55.9 1.3 %collective-permute-start.5 = (f32[6,128,128]{2,1,0:T(8,128)S(1)}, f32[6,128,128]{2,1,0:T(8,128)S(1)}, u32[]{:S(2)}, u32[]{:S(2)}) collective-permute-start(f32[6,128,128]{2,1,0:T(8,128)S(1)} %branch_0_fun.10.kept), channel_id=1, source_target_pairs={{0,16},{1,17},{2,18},{3,19},{4,20},{5,21},{6,22},{7,23},{8,24},{9,... | collective-permute-start | bytes 1179656 | tf_op jit(solution)/shard_map/cond/branch_0_fun/ppermute | solution.py:441
  57.2 7.6 %collective-permute-done.6.got = f32[2,1024,128]{2,1,0:T(8,128)S(1)} collective-permute-done((f32[2,1024,128]{2,1,0:T(8,128)S(1)}, f32[2,1024,128]{2,1,0:T(8,128)S(1)}, u32[]{:S(2)}, u32[]{:S(2)}) %collective-permute-start.6) | collective-permute-done | bytes 1048608 | tf_op jit(solution)/shard_map/cond/branch_0_fun/ppermute | solution.py:451
  64.7 0.6 branch_0_fun.12.kept
  65.4 1.3 %collective-permute-start.7 = (f32[1,128,128]{2,1,0:T(8,128)S(1)}, f32[1,128,128]{2,1,0:T(8,128)S(1)}, u32[]{:S(2)}, u32[]{:S(2)}) collective-permute-start(f32[1,128,128]{2,1,0:T(8,128)S(1)} %branch_0_fun.12.kept), channel_id=1, source_target_pairs={{0,16},{1,17},{2,18},{3,19},{4,20},{5,21},{6,22},{7,23},{8,24},{9,... | collective-permute-start | bytes 196616 | tf_op jit(solution)/shard_map/cond/branch_0_fun/ppermute | solution.py:441
  66.7 0.0 collective-permute-done.1.refs_1_
  66.7 0.0 collective-permute-done.refs_0_
  66.7 0.0 collective-permute-done.3.refs_4_
  66.7 4.2 %branch_0_fun.9 = (f32[512,1024]{1,0:T(8,128)}, f32[3,128,128]{2,1,0:T(8,128)S(1)}) custom-call(s32[1]{0:T(128)} %get-tuple-element.48.window, f32[23,128,128]{2,1,0:T(8,128)S(1)} %get-tuple-element.55.refs_0_.own0, f32[10,128,128]{2,1,0:T(8,128)S(1)} %get-tuple-element.56.own1, f32[10,128,128]{2,1,0:T(8,128)S(1)} %collective-permute-done.refs_0_, ...), custom_call_target="tpu_custom_call" | custom-call | flops 1000000000 | bytes 12582912 | tf_op jit(solution)/shard_map/cond/branch_0_fun/pallas_call | solution.py:483
  70.9 0.0 collective-permute-done.5.came
  70.9 2.1 %branch_0_fun.11 = (f32[512,1024]{1,0:T(8,128)}, f32[1,128,128]{2,1,0:T(8,128)S(1)}) custom-call(s32[1]{0:T(128)} %get-tuple-element.48.window, f32[512,1024]{1,0:T(8,128)} %get-tuple-element.64.old, f32[3,128,128]{2,1,0:T(8,128)S(1)} %get-tuple-element.65.edge, f32[6,128,128]{2,1,0:T(8,128)S(1)} %branch_0_fun.10.kept, ...), custom_call_target="tpu_custom_call", output_to_operand_aliasing={{0}: (1, {})} | custom-call | flops 10000000 | bytes 393216 | tf_op jit(solution)/shard_map/cond/branch_0_fun/pallas_call | solution.py:486
  73.0 0.0 collective-permute-done.7.came
  73.0 1.5 %branch_0_fun.13 = f32[512,1024]{1,0:T(8,128)} custom-call(s32[1]{0:T(128)} %get-tuple-element.48.window, f32[512,1024]{1,0:T(8,128)} %get-tuple-element.67.old, f32[1,128,128]{2,1,0:T(8,128)S(1)} %get-tuple-element.68.ready, f32[1,128,128]{2,1,0:T(8,128)S(1)} %branch_0_fun.12.kept, ...), custom_call_target="tpu_custom_call", output_to_operand_aliasing={{}: (1, {})} | custom-call | flops 10000000 | bytes 393216 | tf_op jit(solution)/shard_map/cond/branch_0_fun/pallas_call | solution.py:499
  (2 shorter events, 0.0 us)
Async XLA Ops:
  0.7 4.7 %copy-start = (f32[2,1024,1024]{2,1,0:T(8,128)S(1)}, f32[2,1024,1024]{2,1,0:T(8,128)}, u32[]{:S(2)}) copy-start(f32[2,1024,1024]{2,1,0:T(8,128)} %get-tuple-element.170.g_ref) | copy-start | bytes 25165828 | tf_op jit(solution)/shard_map/cond
  0.7 4.7 %copy-start.4 = (s32[8]{0:T(128)S(1)}, s32[8]{0:T(128)}, u32[]{:S(2)}) copy-start(s32[8]{0:T(128)} %get-tuple-element.66.counts.counts_ref) | copy-start | bytes 100 | tf_op jit(solution)/shard_map/cond
  0.7 4.7 %copy-start.8 = (f32[5,128]{1,0:T(8,128)S(1)}, f32[5,128]{1,0:T(8,128)}, u32[]{:S(2)}) copy-start(f32[5,128]{1,0:T(8,128)} %get-tuple-element.166.table) | copy-start | bytes 7684 | tf_op jit(solution)/shard_map/cond
  0.7 4.7 %copy-start.12 = (s32[4]{0:T(128)S(1)}, s32[4]{0:T(128)}, u32[]{:S(2)}) copy-start(s32[4]{0:T(128)} %get-tuple-element.162.pops) | copy-start | bytes 52 | tf_op jit(solution)/shard_map/cond
  2.5 28.5 %collective-permute-start.2 = (f32[2,1024,256]{2,1,0:T(8,128)S(1)}, f32[2,1024,256]{2,1,0:T(8,128)S(1)}, u32[]{:S(2)}, u32[]{:S(2)}) collective-permute-start(f32[2,1024,256]{2,1,0:T(8,128)S(1)} %piece.4), channel_id=1, source_target_pairs={{1,0},{2,1},{3,2},{4,3},{5,4},{6,5},{7,6},{8,7},{9,8},{10,9},{11,1... | collective-permute-start | bytes 6291464 | tf_op jit(solution)/shard_map/cond/branch_0_fun/ppermute | solution.py:451
  23.1 30.4 %collective-permute-start.4 = (f32[2,1024,256]{2,1,0:T(8,128)S(1)}, f32[2,1024,256]{2,1,0:T(8,128)S(1)}, u32[]{:S(2)}, u32[]{:S(2)}) collective-permute-start(f32[2,1024,256]{2,1,0:T(8,128)S(1)} %slice_multiply_fusion), channel_id=1, source_target_pairs={{1,0},{2,1},{3,2},{4,3},{5,4},{6,5},{7,6},{8,7},{9,8},{10,9},{11,1... | collective-permute-start | bytes 6291464 | tf_op jit(solution)/shard_map/cond/branch_0_fun/ppermute | solution.py:451
  25.2 39.5 %collective-permute-start.6 = (f32[2,1024,128]{2,1,0:T(8,128)S(1)}, f32[2,1024,128]{2,1,0:T(8,128)S(1)}, u32[]{:S(2)}, u32[]{:S(2)}) collective-permute-start(f32[2,1024,128]{2,1,0:T(8,128)S(1)} %slice_multiply_fusion.1), channel_id=1, source_target_pairs={{1,0},{2,1},{3,2},{4,3},{5,4},{6,5},{7,6},{8,7},{9,8},{10,9},{11,1... | collective-permute-start | bytes 3145736 | tf_op jit(solution)/shard_map/cond/branch_0_fun/ppermute | solution.py:451
  27.7 38.9 %collective-permute-start = (f32[10,128,128]{2,1,0:T(8,128)S(1)}, f32[10,128,128]{2,1,0:T(8,128)S(1)}, u32[]{:S(2)}, u32[]{:S(2)}) collective-permute-start(f32[10,128,128]{2,1,0:T(8,128)S(1)} %get-tuple-element.57), channel_id=1, source_target_pairs={{0,16},{16,0},{1,17},{17,1},{2,18},{18,2},{3,19},{19,3},{4,20},{20... | collective-permute-start | bytes 1966088 | tf_op jit(solution)/shard_map/cond/branch_0_fun/ppermute | solution.py:441
  34.5 32.2 %collective-permute-start.3 = (f32[8,128,128]{2,1,0:T(8,128)S(1)}, f32[8,128,128]{2,1,0:T(8,128)S(1)}, u32[]{:S(2)}, u32[]{:S(2)}) collective-permute-start(f32[8,128,128]{2,1,0:T(8,128)S(1)} %get-tuple-element.63), channel_id=1, source_target_pairs={{0,16},{16,0},{1,17},{17,1},{2,18},{18,2},{3,19},{19,3},{4,20},{20... | collective-permute-start | bytes 1572872 | tf_op jit(solution)/shard_map/cond/branch_0_fun/ppermute | solution.py:441
  34.8 31.9 %collective-permute-start.1 = (f32[7,128,128]{2,1,0:T(8,128)S(1)}, f32[7,128,128]{2,1,0:T(8,128)S(1)}, u32[]{:S(2)}, u32[]{:S(2)}) collective-permute-start(f32[7,128,128]{2,1,0:T(8,128)S(1)} %get-tuple-element.58), channel_id=1, source_target_pairs={{16,0},{17,1},{18,2},{19,3},{20,4},{21,5},{22,6},{23,7},{24,8},{25... | collective-permute-start | bytes 1376264 | tf_op jit(solution)/shard_map/cond/branch_0_fun/ppermute | solution.py:441
  55.9 15.1 %collective-permute-start.5 = (f32[6,128,128]{2,1,0:T(8,128)S(1)}, f32[6,128,128]{2,1,0:T(8,128)S(1)}, u32[]{:S(2)}, u32[]{:S(2)}) collective-permute-start(f32[6,128,128]{2,1,0:T(8,128)S(1)} %branch_0_fun.10.kept), channel_id=1, source_target_pairs={{0,16},{1,17},{2,18},{3,19},{4,20},{5,21},{6,22},{7,23},{8,24},{9,... | collective-permute-start | bytes 1179656 | tf_op jit(solution)/shard_map/cond/branch_0_fun/ppermute | solution.py:441
  65.4 7.7 %collective-permute-start.7 = (f32[1,128,128]{2,1,0:T(8,128)S(1)}, f32[1,128,128]{2,1,0:T(8,128)S(1)}, u32[]{:S(2)}, u32[]{:S(2)}) collective-permute-start(f32[1,128,128]{2,1,0:T(8,128)S(1)} %branch_0_fun.12.kept), channel_id=1, source_target_pairs={{0,16},{1,17},{2,18},{3,19},{4,20},{5,21},{6,22},{7,23},{8,24},{9,... | collective-permute-start | bytes 196616 | tf_op jit(solution)/shard_map/cond/branch_0_fun/ppermute | solution.py:441

commit v4 on v3

--- a/solution.py
+++ b/solution.py
@@ -17,7 +17,7 @@
 SMEM = pl.BlockSpec(memory_space=pltpu.SMEM)
 VMEM = pl.BlockSpec(memory_space=pltpu.VMEM)
 PARAMS = pltpu.CompilerParams(vmem_limit_bytes=20 * 2**20)
-HOPS = {8: (2, 2, 2, 1, 1), 7: (2, 2, 2, 1), 6: (2, 2, 1, 1), 5: (2, 2, 1)}
+HOPS = {8: (2, 2, 2, 1, 1), 7: (2, 2, 1, 1, 1), 6: (2, 2, 1, 1), 5: (2, 2, 1)}
 
 
 class Hop:
@@ -28,6 +28,12 @@
         self.top = max(0, tiles // 2 - self.first) * wide
         self.bottom = (tiles - self.base) * wide
         self.rest = (0, 0)
+        self.skip = 0
+
+    def spot(self, row, base, w):
+        if self.skip:
+            return (row - base) * self.wide + self.wide - 1 - w - self.skip
+        return (row - base) * self.wide + w
 
 
 class Plan:
@@ -44,10 +50,13 @@
             tile += wide
         assert self.hops[-2].first >= self.half
         assert self.hops[-1].first == tiles - 1 and self.hops[-1].wide == 1
+        self.hops[-2].skip = self.hops[-2].wide - 1
+        self.hops[-2].bottom -= self.hops[-2].skip
         spare = sum(max(0, hop.bottom - hop.top) for hop in self.hops[:-2])
         self.first_swap = max(self.n1, self.n0 - spare)
         self.even = self.n1 if steps == min(HOPS) else self.first_swap
         self.extra = self.first_swap - self.even
+        self.late = self.hops[-2].wide > 1
         left = self.first_swap
         for hop in self.hops[:-2]:
             take = max(0, min(self.n0 - left, hop.bottom - hop.top))
@@ -235,8 +244,15 @@
             def put(out, base, owner):
                 for w in range(wide):
                     tile = prod[k * TILE : (k + 1) * TILE, w * TILE : (w + 1) * TILE]
-                    spot = (row + k - base) * wide + w
-                    out[spot] = tile
+                    spot = hop.spot(row + k, base, w)
+                    if hop.skip:
+
+                        @pl.when(spot >= 0)
+                        def _():
+                            out[spot] = tile
+
+                    else:
+                        out[spot] = tile
                     if send is not None:
 
                         @pl.when(group == owner)
@@ -248,14 +264,14 @@
                 pl.when(upper)(functools.partial(put, top, hop.first, 1))
             pl.when(row + k >= hop.base)(functools.partial(put, bottom, hop.base, 0))
 
-    even = hop.first // 2
+    tall = min(wide, 2)
 
     def pair(q, carry):
-        block(2 * q, 2)
+        block(tall * q, tall)
         return carry
 
     if plan.tiles - hop.first > 1:
-        lax.fori_loop(even, plan.tiles // 2, pair, 0)
+        lax.fori_loop(hop.first // tall, plan.tiles // tall, pair, 0)
     else:
         block(hop.first, 1)
     if hop.rest[1]:
@@ -362,7 +378,7 @@
         row = plan.hops[-2].first + i
         edge[i] = band[row - plan.half, plan.tiles + plan.hops[-2].tile - row - 1]
 
-    strip = 64
+    strip = TILE
     strips = TILE // strip
 
     def line(i, carry):
@@ -398,7 +414,8 @@
             step = plan.tiles + hop.tile - row
             tiles = [edge[i]]
             for w in range(min(hop.wide, plan.steps + 1 - step)):
-                tiles.append(kept[i * hop.wide + w] + came[i * hop.wide + w])
+                spot = hop.spot(i, 0, w)
+                tiles.append(kept[spot] + came[spot])
             tiles = skew(tiles, 0)
             for m, tile in enumerate(band_tiles(tiles, step - 1, 0, window[0])):
                 fresh[i, :, m * TILE : (m + 1) * TILE] = tile
@@ -421,7 +438,8 @@
 
     @pl.when(lax.axis_index("pop") == 1)
     def _():
-        tiles = [ready[0]] + skew([kept[0] + came[0]], 0)
+        total = kept[0] + came[0] if plan.late else came[0, 0] + came[1, 0]
+        tiles = [ready[0]] + skew([total], 0)
         (fresh[...],) = band_tiles(tiles, plan.steps - 1, 0, window[0])
         corner = out.at[pl.ds((plan.half - 1) * TILE, TILE), pl.ds((plan.steps - 1) * TILE, TILE)]
         copy = pltpu.make_async_copy(fresh, corner, sem)
@@ -460,7 +478,10 @@
     for j, (hop, got) in enumerate(zip(plan.hops, arrivals)):
         top, bottom, send = hop_part(plan, hop, got, ah, al, own0, j)
         route = both if hop.top or hop.rest[1] else both[:1]
-        parts.append((top, bottom, swap(send, route)))
+        if j + 1 < len(plan.hops) or plan.late:
+            parts.append((top, bottom, swap(send, route)))
+        else:
+            parts.append((top, bottom, lax.all_gather(bottom, "pop")))
     lists = [own0, own1, *swapped]
     for part in parts[:-2]:
         lists += [x for x in part if x is not None]
@@ -475,7 +496,7 @@
         scratch_shapes=[
             pltpu.VMEM((half, steps + 1, TILE, TILE), F32),
             pltpu.VMEM((half * TILE, WIN), F32),
-            pltpu.SemaphoreType.DMA((2 * half,)),
+            pltpu.SemaphoreType.DMA((half,)),
         ],
         cost_estimate=pl.CostEstimate(flops=10**9, bytes_accessed=6 * half * TILE * WIN * 4, transcendentals=0),
         compiler_params=PARAMS,

time: 75.6 us -> 75 us (level)
  transfers between devices with their start and end apart: 8 -> 8, of which waited for: 3 -> 3; matrix products, arithmetic and copies ran while one was open for 1% -> 1% of each run, Pallas kernels for 40% -> 39%
where the time goes in v4:
time: 75 us; the launch traced here: 74.7 us
  Pallas kernels  32.7 us (44%)
  waiting for transfers between devices  26.3 us (35%)
  starting transfers between devices  13.4 us (18%)
  between operations  0.9 us (1%)
  loops' own time  0.79 us (1%)
    ppermute x3, waiting for transfers between devices, band(): arrivals.append(lax.ppermute(piece, 'snp', behind))  26.3 us
    pallas_call x1, Pallas kernels, own_part(): pl.pallas_call(functools.partial(own_kernel, plan), grid=(snps // span,),...  17.3 us
    ppermute x3, starting transfers between devices, band(): arrivals.append(lax.ppermute(piece, 'snp', behind))  7.28 us
    pallas_call x3, Pallas kernels, hop_part(): pl.pallas_call(functools.partial(hop_kernel, plan, hop), in_specs=[VMEM]...  6.44 us
    ppermute x5, starting transfers between devices, swap(): return lax.ppermute(block, 'pop', route)  6.11 us
    pallas_call x1, Pallas kernels, band(): out, edge = finish(window, *lists)  3.6 us
    pallas_call x1, Pallas kernels, band(): pl.pallas_call(functools.partial(next_kernel, plan), in_specs=[SMEM, anyw...  2.07 us
    pallas_call x1, Pallas kernels, piece_part(): pl.pallas_call(piece_kernel, in_specs=[pl.BlockSpec(memory_space=pl.ANY)]...  1.77 us
  transfers between devices with their start and end apart: 8, of which 3 were waited for; matrix products, arithmetic and copies ran while one was open for 1% of the time, Pallas kernels for 39%

profile of v4, /device:TPU:7, one launch (start us, length us, event | category | flops | bytes accessed | tf_op | source)
XLA Modules:
  0.0 74.7 jit_solution(4123724127433716166)
XLA Ops:
  0.7 73.8 %conditional.1 = (f32[512,1024]{1,0:T(8,128)}) conditional(s32[]{:T(128)} %clamp.3, (s32[8]{0:T(128)}, s32[4]{0:T(128)}, f32[5,128]{1,0:T(8,128)}, f32[2,1024,1024]{2,1,0:T(8,128)}, s32[1]{0:T(128)}) %tuple.30, (s32[8]{0:T(128)}, s32[4]{0:T(128)}, f32[5,128]{1,0:T(8,128)}, f32[2,1024,1024]{2,1,0:T(8,128)}, ...), branch_computations={%region_0.1_spmd, %region_1.2_spmd, %region_2.3_spmd, %region_3.4_... | conditional | flops 16927375360 | bytes 124739560 | solution.py:543
  0.7 0.0 copy-start
  0.7 0.0 copy-start.4
  0.7 0.0 copy-start.8
  0.7 0.0 copy-start.12
  0.7 1.8 %piece.4 = f32[2,1024,256]{2,1,0:T(8,128)S(1)} custom-call(s32[8]{0:T(128)} %get-tuple-element.66.counts.counts_ref, f32[2,1024,1024]{2,1,0:T(8,128)} %get-tuple-element.173.g_ref), custom_call_target="tpu_custom_call" | custom-call | flops 1000000 | bytes 4194304 | tf_op jit(solution)/shard_map/cond/branch_0_fun/piece/pallas_call | solution.py:112
  2.5 2.8 %collective-permute-start.2 = (f32[2,1024,256]{2,1,0:T(8,128)S(1)}, f32[2,1024,256]{2,1,0:T(8,128)S(1)}, u32[]{:S(2)}, u32[]{:S(2)}) collective-permute-start(f32[2,1024,256]{2,1,0:T(8,128)S(1)} %piece.4), channel_id=1, source_target_pairs={{1,0},{2,1},{3,2},{4,3},{5,4},{6,5},{7,6},{8,7},{9,8},{10,9},{11,1... | collective-permute-start | bytes 6291464 | tf_op jit(solution)/shard_map/cond/branch_0_fun/ppermute | solution.py:469
  5.4 0.0 copy-done
  5.4 0.0 copy-done.4
  5.4 0.0 copy-done.8
  5.4 0.0 copy-done.12
  5.4 17.3 %branch_0_fun.7 = (bf16[1024,2048]{1,0:T(8,128)(2,1)S(1)}, bf16[1024,2048]{1,0:T(8,128)(2,1)S(1)}, f32[23,128,128]{2,1,0:T(8,128)S(1)}, f32[10,128,128]{2,1,0:T(...) custom-call(s32[8]{0:T(128)S(1)} %copy-done.4, s32[4]{0:T(128)S(1)} %copy-done.12, ...), custom_call_target="tpu_custom_call" | custom-call | flops 8053063680 | bytes 8388608 | tf_op jit(solution)/shard_map/cond/branch_0_fun/pallas_call | solution.py:199
  22.7 0.1 convert_bitcast_fusion
  22.8 0.3 slice_multiply_fusion
  23.1 1.9 %collective-permute-start.4 = (f32[2,1024,256]{2,1,0:T(8,128)S(1)}, f32[2,1024,256]{2,1,0:T(8,128)S(1)}, u32[]{:S(2)}, u32[]{:S(2)}) collective-permute-start(f32[2,1024,256]{2,1,0:T(8,128)S(1)} %slice_multiply_fusion), channel_id=1, source_target_pairs={{1,0},{2,1},{3,2},{4,3},{5,4},{6,5},{7,6},{8,7},{9,8},{10,9},{11,1... | collective-permute-start | bytes 6291464 | tf_op jit(solution)/shard_map/cond/branch_0_fun/ppermute | solution.py:469
  25.0 0.1 slice_multiply_fusion.1
  25.2 2.5 %collective-permute-start.6 = (f32[2,1024,128]{2,1,0:T(8,128)S(1)}, f32[2,1024,128]{2,1,0:T(8,128)S(1)}, u32[]{:S(2)}, u32[]{:S(2)}) collective-permute-start(f32[2,1024,128]{2,1,0:T(8,128)S(1)} %slice_multiply_fusion.1), channel_id=1, source_target_pairs={{1,0},{2,1},{3,2},{4,3},{5,4},{6,5},{7,6},{8,7},{9,8},{10,9},{11,1... | collective-permute-start | bytes 3145736 | tf_op jit(solution)/shard_map/cond/branch_0_fun/ppermute | solution.py:469
  27.7 0.1 collective-permute-start
  27.8 3.2 %collective-permute-done.2.got = f32[2,1024,256]{2,1,0:T(8,128)S(1)} collective-permute-done((f32[2,1024,256]{2,1,0:T(8,128)S(1)}, f32[2,1024,256]{2,1,0:T(8,128)S(1)}, u32[]{:S(2)}, u32[]{:S(2)}) %collective-permute-start.2) | collective-permute-done | bytes 2097184 | tf_op jit(solution)/shard_map/cond/branch_0_fun/ppermute | solution.py:469
  31.0 3.4 %branch_0_fun.8 = (f32[2,128,128]{2,1,0:T(8,128)S(1)}, f32[8,128,128]{2,1,0:T(8,128)S(1)}, f32[8,128,128]{2,1,0:T(8,128)S(1)}) custom-call(f32[2,1024,256]{2,1,0:T(8,128)S(1)} %collective-permute-done.2.got, bf16[1024,2048]{1,0:T(8,128)(2,1)S(1)} %get-tuple-element.59.ah, bf16[1024,2048]{1,0:T(8,128)(2,1)S(1)} %get-tuple-element.60.al, ...), custom_call_target="tpu_custom_call" | custom-call | flops 2013265920 | bytes 2097152 | tf_op jit(solution)/shard_map/cond/branch_0_fun/pallas_call | solution.py:289
  34.5 0.3 collective-permute-start.3
  34.8 3.1 %collective-permute-start.1 = (f32[7,128,128]{2,1,0:T(8,128)S(1)}, f32[7,128,128]{2,1,0:T(8,128)S(1)}, u32[]{:S(2)}, u32[]{:S(2)}) collective-permute-start(f32[7,128,128]{2,1,0:T(8,128)S(1)} %get-tuple-element.58), channel_id=1, source_target_pairs={{16,0},{17,1},{18,2},{19,3},{20,4},{21,5},{22,6},{23,7},{24,8},{25... | collective-permute-start | bytes 1376264 | tf_op jit(solution)/shard_map/cond/branch_0_fun/ppermute | solution.py:459
  37.9 15.6 %collective-permute-done.4.got = f32[2,1024,256]{2,1,0:T(8,128)S(1)} collective-permute-done((f32[2,1024,256]{2,1,0:T(8,128)S(1)}, f32[2,1024,256]{2,1,0:T(8,128)S(1)}, u32[]{:S(2)}, u32[]{:S(2)}) %collective-permute-start.4) | collective-permute-done | bytes 2097184 | tf_op jit(solution)/shard_map/cond/branch_0_fun/ppermute | solution.py:469
  53.5 2.4 %branch_0_fun.10.kept = f32[5,128,128]{2,1,0:T(8,128)S(1)} custom-call(f32[2,1024,256]{2,1,0:T(8,128)S(1)} %collective-permute-done.4.got, bf16[1024,2048]{1,0:T(8,128)(2,1)S(1)} %get-tuple-element.59.ah, bf16[1024,2048]{1,0:T(8,128)(2,1)S(1)} %get-tuple-element.60.al), custom_call_target="tpu_custom_call" | custom-call | flops 1207959552 | bytes 2097152 | tf_op jit(solution)/shard_map/cond/branch_0_fun/pallas_call | solution.py:289
  55.9 1.3 %collective-permute-start.5 = (f32[5,128,128]{2,1,0:T(8,128)S(1)}, f32[5,128,128]{2,1,0:T(8,128)S(1)}, u32[]{:S(2)}, u32[]{:S(2)}) collective-permute-start(f32[5,128,128]{2,1,0:T(8,128)S(1)} %branch_0_fun.10.kept), channel_id=1, source_target_pairs={{0,16},{1,17},{2,18},{3,19},{4,20},{5,21},{6,22},{7,23},{8,24},{9,... | collective-permute-start | bytes 983048 | tf_op jit(solution)/shard_map/cond/branch_0_fun/ppermute | solution.py:459
  57.2 7.5 %collective-permute-done.6.got = f32[2,1024,128]{2,1,0:T(8,128)S(1)} collective-permute-done((f32[2,1024,128]{2,1,0:T(8,128)S(1)}, f32[2,1024,128]{2,1,0:T(8,128)S(1)}, u32[]{:S(2)}, u32[]{:S(2)}) %collective-permute-start.6) | collective-permute-done | bytes 1048608 | tf_op jit(solution)/shard_map/cond/branch_0_fun/ppermute | solution.py:469
  64.7 0.6 branch_0_fun.12.kept
  65.4 1.3 %collective-permute-start.7 = (f32[1,128,128]{2,1,0:T(8,128)S(1)}, f32[1,128,128]{2,1,0:T(8,128)S(1)}, u32[]{:S(2)}, u32[]{:S(2)}) collective-permute-start(f32[1,128,128]{2,1,0:T(8,128)S(1)} %branch_0_fun.12.kept), channel_id=1, source_target_pairs={{0,16},{1,17},{2,18},{3,19},{4,20},{5,21},{6,22},{7,23},{8,24},{9,... | collective-permute-start | bytes 196616 | tf_op jit(solution)/shard_map/cond/branch_0_fun/ppermute | solution.py:459
  66.7 0.0 collective-permute-done.1.refs_1_
  66.7 0.0 collective-permute-done.refs_0_
  66.7 0.0 collective-permute-done.3.refs_4_
  66.7 3.6 %branch_0_fun.9 = (f32[512,1024]{1,0:T(8,128)}, f32[3,128,128]{2,1,0:T(8,128)S(1)}) custom-call(s32[1]{0:T(128)} %get-tuple-element.48.window, f32[23,128,128]{2,1,0:T(8,128)S(1)} %get-tuple-element.55.refs_0_.own0, f32[10,128,128]{2,1,0:T(8,128)S(1)} %get-tuple-element.56.own1, f32[10,128,128]{2,1,0:T(8,128)S(1)} %collective-permute-done.refs_0_, ...), custom_call_target="tpu_custom_call" | custom-call | flops 1000000000 | bytes 12582912 | tf_op jit(solution)/shard_map/cond/branch_0_fun/pallas_call | solution.py:504
  70.3 0.0 collective-permute-done.5.came
  70.3 2.1 %branch_0_fun.11 = (f32[512,1024]{1,0:T(8,128)}, f32[1,128,128]{2,1,0:T(8,128)S(1)}) custom-call(s32[1]{0:T(128)} %get-tuple-element.48.window, f32[512,1024]{1,0:T(8,128)} %get-tuple-element.64.old, f32[3,128,128]{2,1,0:T(8,128)S(1)} %get-tuple-element.65.edge, f32[5,128,128]{2,1,0:T(8,128)S(1)} %branch_0_fun.10.kept, ...), custom_call_target="tpu_custom_call", output_to_operand_aliasing={{0}: (1, {})} | custom-call | flops 10000000 | bytes 393216 | tf_op jit(solution)/shard_map/cond/branch_0_fun/pallas_call | solution.py:507
  72.4 0.0 collective-permute-done.7.came
  72.4 1.5 %branch_0_fun.13 = f32[512,1024]{1,0:T(8,128)} custom-call(s32[1]{0:T(128)} %get-tuple-element.48.window, f32[512,1024]{1,0:T(8,128)} %get-tuple-element.67.old, f32[1,128,128]{2,1,0:T(8,128)S(1)} %get-tuple-element.68.ready, f32[1,128,128]{2,1,0:T(8,128)S(1)} %branch_0_fun.12.kept, ...), custom_call_target="tpu_custom_call", output_to_operand_aliasing={{}: (1, {})} | custom-call | flops 10000000 | bytes 393216 | tf_op jit(solution)/shard_map/cond/branch_0_fun/pallas_call | solution.py:520
  (2 shorter events, 0.0 us)
Async XLA Ops:
  0.7 4.7 %copy-start = (f32[2,1024,1024]{2,1,0:T(8,128)S(1)}, f32[2,1024,1024]{2,1,0:T(8,128)}, u32[]{:S(2)}) copy-start(f32[2,1024,1024]{2,1,0:T(8,128)} %get-tuple-element.173.g_ref) | copy-start | bytes 25165828 | tf_op jit(solution)/shard_map/cond
  0.7 4.7 %copy-start.4 = (s32[8]{0:T(128)S(1)}, s32[8]{0:T(128)}, u32[]{:S(2)}) copy-start(s32[8]{0:T(128)} %get-tuple-element.66.counts.counts_ref) | copy-start | bytes 100 | tf_op jit(solution)/shard_map/cond
  0.7 4.7 %copy-start.8 = (f32[5,128]{1,0:T(8,128)S(1)}, f32[5,128]{1,0:T(8,128)}, u32[]{:S(2)}) copy-start(f32[5,128]{1,0:T(8,128)} %get-tuple-element.169.table) | copy-start | bytes 7684 | tf_op jit(solution)/shard_map/cond
  0.7 4.7 %copy-start.12 = (s32[4]{0:T(128)S(1)}, s32[4]{0:T(128)}, u32[]{:S(2)}) copy-start(s32[4]{0:T(128)} %get-tuple-element.165.pops) | copy-start | bytes 52 | tf_op jit(solution)/shard_map/cond
  2.5 28.5 %collective-permute-start.2 = (f32[2,1024,256]{2,1,0:T(8,128)S(1)}, f32[2,1024,256]{2,1,0:T(8,128)S(1)}, u32[]{:S(2)}, u32[]{:S(2)}) collective-permute-start(f32[2,1024,256]{2,1,0:T(8,128)S(1)} %piece.4), channel_id=1, source_target_pairs={{1,0},{2,1},{3,2},{4,3},{5,4},{6,5},{7,6},{8,7},{9,8},{10,9},{11,1... | collective-permute-start | bytes 6291464 | tf_op jit(solution)/shard_map/cond/branch_0_fun/ppermute | solution.py:469
  23.1 30.4 %collective-permute-start.4 = (f32[2,1024,256]{2,1,0:T(8,128)S(1)}, f32[2,1024,256]{2,1,0:T(8,128)S(1)}, u32[]{:S(2)}, u32[]{:S(2)}) collective-permute-start(f32[2,1024,256]{2,1,0:T(8,128)S(1)} %slice_multiply_fusion), channel_id=1, source_target_pairs={{1,0},{2,1},{3,2},{4,3},{5,4},{6,5},{7,6},{8,7},{9,8},{10,9},{11,1... | collective-permute-start | bytes 6291464 | tf_op jit(solution)/shard_map/cond/branch_0_fun/ppermute | solution.py:469
  25.2 39.5 %collective-permute-start.6 = (f32[2,1024,128]{2,1,0:T(8,128)S(1)}, f32[2,1024,128]{2,1,0:T(8,128)S(1)}, u32[]{:S(2)}, u32[]{:S(2)}) collective-permute-start(f32[2,1024,128]{2,1,0:T(8,128)S(1)} %slice_multiply_fusion.1), channel_id=1, source_target_pairs={{1,0},{2,1},{3,2},{4,3},{5,4},{6,5},{7,6},{8,7},{9,8},{10,9},{11,1... | collective-permute-start | bytes 3145736 | tf_op jit(solution)/shard_map/cond/branch_0_fun/ppermute | solution.py:469
  27.7 38.9 %collective-permute-start = (f32[10,128,128]{2,1,0:T(8,128)S(1)}, f32[10,128,128]{2,1,0:T(8,128)S(1)}, u32[]{:S(2)}, u32[]{:S(2)}) collective-permute-start(f32[10,128,128]{2,1,0:T(8,128)S(1)} %get-tuple-element.57), channel_id=1, source_target_pairs={{0,16},{16,0},{1,17},{17,1},{2,18},{18,2},{3,19},{19,3},{4,20},{20... | collective-permute-start | bytes 1966088 | tf_op jit(solution)/shard_map/cond/branch_0_fun/ppermute | solution.py:459
  34.5 32.2 %collective-permute-start.3 = (f32[8,128,128]{2,1,0:T(8,128)S(1)}, f32[8,128,128]{2,1,0:T(8,128)S(1)}, u32[]{:S(2)}, u32[]{:S(2)}) collective-permute-start(f32[8,128,128]{2,1,0:T(8,128)S(1)} %get-tuple-element.63), channel_id=1, source_target_pairs={{0,16},{16,0},{1,17},{17,1},{2,18},{18,2},{3,19},{19,3},{4,20},{20... | collective-permute-start | bytes 1572872 | tf_op jit(solution)/shard_map/cond/branch_0_fun/ppermute | solution.py:459
  34.8 31.9 %collective-permute-start.1 = (f32[7,128,128]{2,1,0:T(8,128)S(1)}, f32[7,128,128]{2,1,0:T(8,128)S(1)}, u32[]{:S(2)}, u32[]{:S(2)}) collective-permute-start(f32[7,128,128]{2,1,0:T(8,128)S(1)} %get-tuple-element.58), channel_id=1, source_target_pairs={{16,0},{17,1},{18,2},{19,3},{20,4},{21,5},{22,6},{23,7},{24,8},{25... | collective-permute-start | bytes 1376264 | tf_op jit(solution)/shard_map/cond/branch_0_fun/ppermute | solution.py:459
  55.9 14.4 %collective-permute-start.5 = (f32[5,128,128]{2,1,0:T(8,128)S(1)}, f32[5,128,128]{2,1,0:T(8,128)S(1)}, u32[]{:S(2)}, u32[]{:S(2)}) collective-permute-start(f32[5,128,128]{2,1,0:T(8,128)S(1)} %branch_0_fun.10.kept), channel_id=1, source_target_pairs={{0,16},{1,17},{2,18},{3,19},{4,20},{5,21},{6,22},{7,23},{8,24},{9,... | collective-permute-start | bytes 983048 | tf_op jit(solution)/shard_map/cond/branch_0_fun/ppermute | solution.py:459
  65.4 7.0 %collective-permute-start.7 = (f32[1,128,128]{2,1,0:T(8,128)S(1)}, f32[1,128,128]{2,1,0:T(8,128)S(1)}, u32[]{:S(2)}, u32[]{:S(2)}) collective-permute-start(f32[1,128,128]{2,1,0:T(8,128)S(1)} %branch_0_fun.12.kept), channel_id=1, source_target_pairs={{0,16},{1,17},{2,18},{3,19},{4,20},{5,21},{6,22},{7,23},{8,24},{9,... | collective-permute-start | bytes 196616 | tf_op jit(solution)/shard_map/cond/branch_0_fun/ppermute | solution.py:459
